TPU v7x, 8 devices: a whole 2x2x1 slice. The times are simulated.
8 devices in a mesh: data: 8 (over z, y, x, core).
Axes of the slice: x: 2, y: 2, z: 1, core: 2. Of those that a mesh axis runs over, the one named last changes fastest.
Arguments:
- x_in: bfloat16 [32, 128, 384], P('data')
- g_out: bfloat16 [32, 128, 384], P('data')
- step_emb: bfloat16 [6, 384], replicated
- w_q: bfloat16 [384, 6, 64], replicated
- w_k: bfloat16 [384, 6, 64], replicated
- w_v: bfloat16 [384, 6, 64], replicated
- w_o: bfloat16 [6, 64, 384], replicated
- w_up: bfloat16 [384, 1536], replicated
- w_down: bfloat16 [1536, 384], replicated
Outputs:
- output 1: float32 [384, 6, 64], replicated
- output 2: float32 [384, 6, 64], replicated
- output 3: float32 [384, 6, 64], replicated
- output 4: float32 [6, 64, 384], replicated
- output 5: float32 [384, 1536], replicated
- output 6: float32 [1536, 384], replicated
- output 7: bfloat16 [32, 128, 384], P('data')
All inputs are finite; a program needn't handle non-finite values.
Results may differ from a plain program's by a relative error of at most 0.02.
Values are sent between devices in bfloat16 or wider.
A program may use at most 1 GiB of HBM per device.

v0:
```python
import functools
import math

import jax
import jax.numpy as jnp
from jax import lax
from jax.experimental import pallas as pl
from jax.experimental.pallas import tpu as pltpu
from jax.sharding import PartitionSpec as P

EPS = 1e-6
F32 = jnp.float32
BF16 = jnp.bfloat16
LOG2E = math.log2(math.e)
GC0 = math.sqrt(2.0 / math.pi)
GC1 = GC0 * 0.044715
NT = (((1,), (1,)), ((), ()))
TN = (((0,), (0,)), ((), ()))


def mm(a, b):
    return jnp.dot(a, b, preferred_element_type=F32)


def mmg(a, b, dims):
    return lax.dot_general(a, b, dims, preferred_element_type=F32)


def blocks(total, size):
    return [(s, min(size, total - s)) for s in range(0, total, size)]


def rms_scale(xf):
    return lax.rsqrt(jnp.mean(xf * xf, axis=-1, keepdims=True) + EPS)


def norm_back(xf, r, dy):
    inner = jnp.mean(xf * dy, axis=-1, keepdims=True)
    return dy * r - xf * (r * r * r * inner)


def block_kernel(n_seq, seq, n_layers, n_heads,
                 x_ref, g_ref, emb_ref, wq_ref, wk_ref, wv_ref, wo_ref, wup_ref, wdn_ref,
                 gq_ref, gk_ref, gv_ref, go_ref, gup_ref, gdn_ref, dx_ref,
                 wqkv_s, wqkvt_s, wot_s, wupt_s, wdnt_s,
                 x_s, qkv_s, p_s, mix_s, h_s, z_s,
                 u_s, g_s, dup_s, dn_s, dmix_s, dqkv_s, d_s, dmid_s):
    tok, dm = d_s.shape
    ff = wup_ref.shape[1]
    hd = dm // n_heads
    pw = 2 * hd
    n_pair = n_heads // 2
    scale = hd ** -0.5
    RB = 64
    NB = 256
    rows = blocks(tok, RB)

    for i, w in enumerate((wq_ref, wk_ref, wv_ref)):
        wt = w[...]
        wqkvt_s[i * dm:(i + 1) * dm, :] = wt
        wqkv_s[:, i * dm:(i + 1) * dm] = wt.T
    wot_s[...] = wo_ref[...].T
    wupt_s[...] = wup_ref[...].T
    wdnt_s[...] = wdn_ref[...].T
    for ref in (gq_ref, gk_ref, gv_ref, go_ref, gup_ref, gdn_ref):
        ref[...] = jnp.zeros(ref.shape, F32)

    low = lax.broadcasted_iota(jnp.int32, (seq, pw), 1) < hd

    def stack(a):
        zero = jnp.zeros_like(a)
        return jnp.concatenate([jnp.where(low, a, zero), jnp.where(low, zero, a)], axis=0)

    def halves(a):
        return a[:, :seq], a[:, seq:]

    d_s[...] = x_ref[...]

    def fwd(l, carry):
        emb = emb_ref[l]
        for r0, rn in rows:
            rs = slice(r0, r0 + rn)
            xb = (d_s[rs, :].astype(F32) + emb).astype(BF16)
            x_s[l, rs, :] = xb
            xf = xb.astype(F32)
            u_s[rs, :] = (xf * rms_scale(xf)).astype(BF16)
        for n0, nn in blocks(3 * dm, NB):
            ns = slice(n0, n0 + nn)
            qkv_s[l, :, ns] = mm(u_s[...], wqkv_s[:, ns]).astype(BF16)
        for s in range(n_seq):
            rs = slice(s * seq, (s + 1) * seq)
            for j in range(n_pair):
                c = j * pw
                q = qkv_s[l, rs, c:c + pw]
                k = stack(qkv_s[l, rs, dm + c:dm + c + pw])
                v = stack(qkv_s[l, rs, 2 * dm + c:2 * dm + c + pw])
                sc = mmg(q, k, NT).astype(BF16).astype(F32)
                ps = []
                for half in halves(sc):
                    top = jnp.max(half, axis=-1, keepdims=True)
                    e = jnp.exp2((half - top) * (scale * LOG2E))
                    ps.append(e * (1.0 / jnp.sum(e, axis=-1, keepdims=True)))
                p = jnp.concatenate(ps, axis=1)
                p_s[l, s * n_pair + j] = p
                mix_s[l, rs, c:c + pw] = mm(p.astype(BF16), v).astype(BF16)
        for n0, nn in blocks(dm, NB):
            ns = slice(n0, n0 + nn)
            o = mm(mix_s[l], wo_ref[:, ns]).astype(BF16)
            h_s[l, :, ns] = (x_s[l, :, ns].astype(F32) + o.astype(F32)).astype(BF16)
        for r0, rn in rows:
            rs = slice(r0, r0 + rn)
            hf = h_s[l, rs, :].astype(F32)
            u_s[rs, :] = (hf * rms_scale(hf)).astype(BF16)
        for n0, nn in blocks(ff, NB):
            ns = slice(n0, n0 + nn)
            zb = mm(u_s[...], wup_ref[:, ns]).astype(BF16)
            z_s[l, :, ns] = zb
            for r0, rn in rows:
                z = zb[r0:r0 + rn].astype(F32)
                t = jnp.tanh(z * (GC0 + GC1 * (z * z)))
                hz = 0.5 * z
                g_s[r0:r0 + rn, ns] = (hz + hz * t).astype(BF16)
        for n0, nn in blocks(dm, NB):
            ns = slice(n0, n0 + nn)
            y = mm(g_s[...], wdn_ref[:, ns]).astype(BF16)
            d_s[:, ns] = (h_s[l, :, ns].astype(F32) + y.astype(F32)).astype(BF16)
        return carry

    lax.fori_loop(0, n_layers, fwd, 0)
    d_s[...] = g_ref[...]

    def bwd(i, carry):
        l = n_layers - 1 - i
        for n0, nn in blocks(ff, NB):
            ns = slice(n0, n0 + nn)
            da = mm(d_s[...], wdnt_s[:, ns]).astype(BF16)
            for r0, rn in rows:
                rs = slice(r0, r0 + rn)
                z = z_s[l, rs, ns].astype(F32)
                z2 = z * z
                t = jnp.tanh(z * (GC0 + GC1 * z2))
                hz = 0.5 * z
                g_s[rs, ns] = (hz + hz * t).astype(BF16)
                dg = (0.5 + 0.5 * t) + hz * (1.0 - t * t) * (GC0 + 3.0 * GC1 * z2)
                dup_s[rs, ns] = (da[rs].astype(F32) * dg).astype(BF16)
        for n0, nn in blocks(ff, NB):
            gdn_ref[n0:n0 + nn, :] += mmg(g_s[:, n0:n0 + nn], d_s[...], TN)
        for n0, nn in blocks(dm, NB):
            ns = slice(n0, n0 + nn)
            dn_s[:, ns] = mm(dup_s[...], wupt_s[:, ns]).astype(BF16)
        for r0, rn in rows:
            rs = slice(r0, r0 + rn)
            hf = h_s[l, rs, :].astype(F32)
            r = rms_scale(hf)
            u_s[rs, :] = (hf * r).astype(BF16)
            dh = norm_back(hf, r, dn_s[rs, :].astype(F32)).astype(BF16)
            dmid_s[rs, :] = (d_s[rs, :].astype(F32) + dh.astype(F32)).astype(BF16)
        for n0, nn in blocks(ff, NB):
            ns = slice(n0, n0 + nn)
            gup_ref[:, ns] += mmg(u_s[...], dup_s[:, ns], TN)
        for n0, nn in blocks(dm, NB):
            ns = slice(n0, n0 + nn)
            dmix_s[:, ns] = mm(dmid_s[...], wot_s[:, ns]).astype(BF16)
        go_ref[...] += mmg(mix_s[l], dmid_s[...], TN)
        for s in range(n_seq):
            rs = slice(s * seq, (s + 1) * seq)
            for j in range(n_pair):
                c = j * pw
                q = stack(qkv_s[l, rs, c:c + pw])
                k = stack(qkv_s[l, rs, dm + c:dm + c + pw])
                v = stack(qkv_s[l, rs, 2 * dm + c:2 * dm + c + pw])
                dmx = dmix_s[rs, c:c + pw]
                p = p_s[l, s * n_pair + j]
                dp = mmg(dmx, v, NT).astype(BF16).astype(F32)
                dss = []
                for ph, dph in zip(halves(p), halves(dp)):
                    inner = jnp.sum(ph * dph, axis=-1, keepdims=True)
                    dss.append((ph * (dph - inner) * scale).astype(BF16))
                ds = jnp.concatenate(dss, axis=1)
                dst = jnp.concatenate(dss, axis=0)
                pst = jnp.concatenate([a.astype(BF16) for a in halves(p)], axis=0)
                dqkv_s[rs, c:c + pw] = mm(ds, k).astype(BF16)
                dqkv_s[rs, dm + c:dm + c + pw] = mmg(dst, q, TN).astype(BF16)
                dqkv_s[rs, 2 * dm + c:2 * dm + c + pw] = mmg(pst, stack(dmx), TN).astype(BF16)
        for n0, nn in blocks(dm, NB):
            ns = slice(n0, n0 + nn)
            dn_s[:, ns] = mm(dqkv_s[...], wqkvt_s[:, ns]).astype(BF16)
        for r0, rn in rows:
            rs = slice(r0, r0 + rn)
            xf = x_s[l, rs, :].astype(F32)
            r = rms_scale(xf)
            u_s[rs, :] = (xf * r).astype(BF16)
            dh = norm_back(xf, r, dn_s[rs, :].astype(F32)).astype(BF16)
            d_s[rs, :] = (dmid_s[rs, :].astype(F32) + dh.astype(F32)).astype(BF16)
        for i3, ref in enumerate((gq_ref, gk_ref, gv_ref)):
            ref[...] += mmg(dqkv_s[:, i3 * dm:(i3 + 1) * dm], u_s[...], TN)
        return carry

    lax.fori_loop(0, n_layers, bwd, 0)
    dx_ref[...] = d_s[...]


def solution(mesh):
    batch_spec = P('data', None, None)

    def per_device(x_loc, g_loc, step_emb, w_q, w_k, w_v, w_o, w_up, w_down):
        n_seq, seq, dm = x_loc.shape
        n_layers = step_emb.shape[0]
        n_heads, hd = w_q.shape[1:]
        ff = w_up.shape[1]
        tok = n_seq * seq
        n_pair = n_heads // 2
        wts = [w.transpose(1, 2, 0).reshape(n_heads * hd, dm) for w in (w_q, w_k, w_v)]
        vm = pl.BlockSpec(memory_space=pltpu.VMEM)
        sq = jax.ShapeDtypeStruct((dm, dm), F32)
        outs = pl.pallas_call(
            functools.partial(block_kernel, n_seq, seq, n_layers, n_heads),
            out_shape=(sq, sq, sq, sq, jax.ShapeDtypeStruct((dm, ff), F32), jax.ShapeDtypeStruct((ff, dm), F32),
                       jax.ShapeDtypeStruct((tok, dm), BF16)),
            in_specs=[vm] * 9,
            out_specs=[vm] * 7,
            scratch_shapes=[
                pltpu.VMEM((dm, 3 * dm), BF16),
                pltpu.VMEM((3 * dm, dm), BF16),
                pltpu.VMEM((dm, dm), BF16),
                pltpu.VMEM((ff, dm), BF16),
                pltpu.VMEM((dm, ff), BF16),
                pltpu.VMEM((n_layers, tok, dm), BF16),
                pltpu.VMEM((n_layers, tok, 3 * dm), BF16),
                pltpu.VMEM((n_layers, n_seq * n_pair, seq, 2 * seq), F32),
                pltpu.VMEM((n_layers, tok, dm), BF16),
                pltpu.VMEM((n_layers, tok, dm), BF16),
                pltpu.VMEM((n_layers, tok, ff), BF16),
                pltpu.VMEM((tok, dm), BF16),
                pltpu.VMEM((tok, ff), BF16),
                pltpu.VMEM((tok, ff), BF16),
                pltpu.VMEM((tok, dm), BF16),
                pltpu.VMEM((tok, dm), BF16),
                pltpu.VMEM((tok, 3 * dm), BF16),
                pltpu.VMEM((tok, dm), BF16),
                pltpu.VMEM((tok, dm), BF16),
            ],
            compiler_params=pltpu.CompilerParams(vmem_limit_bytes=67043328),
        )(x_loc.reshape(tok, dm), g_loc.reshape(tok, dm), step_emb.astype(F32)[:, None, :],
          *wts, w_o.reshape(n_heads * hd, dm), w_up, w_down)
        sums = lax.psum(tuple(outs[:6]), 'data')
        heads = [a.reshape(n_heads, hd, dm).transpose(2, 0, 1) for a in sums[:3]]
        return (*heads, sums[3].reshape(n_heads, hd, dm), sums[4], sums[5], outs[6].reshape(n_seq, seq, dm))

    return jax.shard_map(per_device, mesh=mesh, in_specs=(batch_spec, batch_spec, P(), P(), P(), P(), P(), P(), P()), out_specs=(P(), P(), P(), P(), P(), P(), batch_spec), check_vma=False)
```

profile of v0, /device:TPU:0, one launch (start us, length us, event | category | flops | bytes accessed | tf_op | source)
XLA Modules:
  0.0 222.5 jit_solution(6611779354363687899)
XLA Ops:
  7.2 0.0 all-reduce.3.cloned.1.call-start
  7.2 1.3 reshape.58.emb_ref
  8.5 93.4 %shard_map.144 = (f32[384,384]{1,0:T(8,128)}, f32[384,384]{1,0:T(8,128)}, f32[384,384]{1,0:T(8,128)}, f32[384,384]{1,0:T(8,128)}, f32[384,1536]{1,0:T(8,128)}, /...) custom-call(bf16[512,384]{1,0:T(8,128)(2,1)} %bitcast.27, bf16[512,384]{1,0:T(8,128)(2,1)} %bitcast.28, ...), custom_call_target="tpu_custom_call" | custom-call | tf_op jit(solution)/shard_map/pallas_call | solution.py:216
  101.9 0.0 all-reduce.3.cloned.1.call-update
  101.9 104.2 %all-reduce.3.cloned.1.call-done = (f32[384,6,64]{0,2,1:T(8,128)}, f32[384,6,64]{0,2,1:T(8,128)}, f32[384,6,64]{0,2,1:T(8,128)}, f32[6,64,384]{2,1,0:T(8,128)}, f32[384,1536]{1,0:T(8,128)}, /*index=5*/f32[1536,384]{1,0:T(8,128)}) async-done(((f32[384,6,64]{0,2,1:T(8,128)}, f32[384,6,64]{0,2,1:T(8,128)}, f32[384,6,64]{0,2,1:T(8,128)}, f32[6,64,384]{2,1,0:T(8,128)}, f32[384,1536]{1,0:T(8,128)}, ...) | async-done | bytes 7077904 | tf_op jit(solution)/shard_map/psum | solution.py:246
  206.1 0.0 copy-start.3
  206.2 0.0 copy-start.2
  206.2 0.0 copy-start.1
  206.2 2.1 copy.22
  208.2 1.9 copy.23
  210.1 0.0 copy-done.3
  210.1 0.8 copy.24
  211.0 0.0 copy-done.2
  211.0 0.8 copy.25
  211.8 0.0 copy-done.1
  211.8 0.0 copy-start
  211.8 1.4 copy.26
  213.2 1.1 copy-done
  214.3 1.4 copy.27
Async XLA Ops:
  7.2 199.0 %all-reduce.3.cloned.1.call-start = ((), (), s32[]{:S(2)}) async-start(), calls=%async_computation | async-start | bytes 14155776 | tf_op jit(solution)/shard_map/psum | solution.py:246
  206.1 4.0 %copy-start.3 = (f32[384,6,64]{0,2,1:T(8,128)S(1)}, f32[384,6,64]{0,2,1:T(8,128)}, u32[]{:S(2)}) copy-start(f32[384,6,64]{0,2,1:T(8,128)} %get-tuple-element.29) | copy-start | bytes 1769476
  206.2 4.8 %copy-start.2 = (f32[6,64,384]{2,1,0:T(8,128)S(1)}, f32[6,64,384]{2,1,0:T(8,128)}, u32[]{:S(2)}) copy-start(f32[6,64,384]{2,1,0:T(8,128)} %get-tuple-element.30) | copy-start | bytes 1769476
  206.2 5.6 %copy-start.1 = (f32[384,1536]{1,0:T(8,128)S(1)}, f32[384,1536]{1,0:T(8,128)}, u32[]{:S(2)}) copy-start(f32[384,1536]{1,0:T(8,128)} %get-tuple-element.31) | copy-start | bytes 7077892
  211.8 2.5 %copy-start = (f32[1536,384]{1,0:T(8,128)S(1)}, f32[1536,384]{1,0:T(8,128)}, u32[]{:S(2)}) copy-start(f32[1536,384]{1,0:T(8,128)} %get-tuple-element.32) | copy-start | bytes 7077892
Sparse Core Ops, SparseCore 0:
  102.0 104.0 all-reduce.2
where the time goes:
time: 223 us
  waiting for transfers between devices  104 us (47%)
  Pallas kernels  93.4 us (42%)
  between operations  14 us (6%)
  local copies, waits for them, and re-layouts  10.8 us (5%)
    psum x1, waiting for transfers between devices, per_device(): sums = lax.psum(tuple(outs[:6]), 'data')  104 us
    pallas_call x1, Pallas kernels, per_device(): pl.pallas_call(functools.partial(block_kernel, n_seq, seq, n_layers, n_he...  93.4 us
    unnamed x14, local copies, waits for them, and re-layouts  9.54 us
  transfers between devices with their start and end apart: 1, of which 1 were waited for; matrix products, arithmetic and copies ran while one was open for 0% of the time, Pallas kernels for 0%

commit v1 on v0

--- a/solution.py
+++ b/solution.py
@@ -11,6 +11,7 @@
 EPS = 1e-6
 F32 = jnp.float32
 BF16 = jnp.bfloat16
+MESH = pl.DeviceIdType.MESH
 LOG2E = math.log2(math.e)
 GC0 = math.sqrt(2.0 / math.pi)
 GC1 = GC0 * 0.044715
@@ -198,6 +199,169 @@
 
     lax.fori_loop(0, n_layers, bwd, 0)
     dx_ref[...] = d_s[...]
+
+
+def reduce_kernel(n_chunk, gq_ref, gk_ref, gv_ref, go_ref, gup_ref, gdn_ref,
+                  oq_ref, ok_ref, ov_ref, oo_ref, oup_ref, odn_ref,
+                  acc, r0, ra, rb, ra2, rb2, in_sem, out_sem, ssem, rsem, free_sem):
+    dm = acc.shape[1]
+    me = lax.axis_index('data')
+    c = lax.rem(me, 2)
+    x = lax.rem(lax.div(me, 2), 2)
+    y = lax.div(me, 4)
+    cp = me + 1 - 2 * c
+    xp = me + 2 - 4 * x
+    yp = me + 4 - 8 * y
+
+    def views(dn, up, o, q, k, v):
+        n = dn.shape[0] // dm
+        return ([dn.at[i * dm:(i + 1) * dm, :] for i in range(n)]
+                + [up.at[:, i * dm:(i + 1) * dm] for i in range(n)] + [o, q, k, v])
+
+    ins = views(gdn_ref, gup_ref, go_ref, gq_ref, gk_ref, gv_ref)
+    outs = views(odn_ref, oup_ref, oo_ref, oq_ref, ok_ref, ov_ref)
+    loads = [pltpu.make_async_copy(src, acc.at[i], in_sem.at[i]) for i, src in enumerate(ins)]
+    for ld in loads:
+        ld.start()
+
+    barrier = pltpu.get_barrier_semaphore()
+    for p in (cp, xp, yp):
+        pl.semaphore_signal(barrier, inc=1, device_id=(p,), device_id_type=MESH)
+    pl.semaphore_wait(barrier, 3)
+
+    h0, h1, h2, h3 = dm // 2, dm // 4, dm // 8, dm // 16
+    own = c * h0
+    oth = (1 - c) * h0
+    a0, a0n = own + x * h2, own + (1 - x) * h2
+    b0, b0n = own + h1 + y * h2, own + h1 + (1 - y) * h2
+    a1, a1n = a0 + y * h3, a0 + (1 - y) * h3
+    b1, b1n = b0 + x * h3, b0 + (1 - x) * h3
+
+    def part(k, off, n):
+        return acc.at[k, pl.ds(pl.multiple_of(off, 8), n), :]
+
+    def send(j, src, dst, dev):
+        def at(k):
+            return pltpu.make_async_remote_copy(
+                src_ref=src(k), dst_ref=dst(k), send_sem=ssem.at[j, k], recv_sem=rsem.at[j, k],
+                device_id=(dev,), device_id_type=MESH)
+        return at
+
+    def rows_of(off, n):
+        return lambda k: part(k, off, n)
+
+    def slot(ref, n):
+        return lambda k: ref.at[k, 0:n, :]
+
+    cs = [
+        send(0, rows_of(oth, h0), slot(r0, h0), cp),
+        send(1, rows_of(a0n, h2), slot(ra, h2), xp),
+        send(2, rows_of(b0n, h2), slot(rb, h2), yp),
+        send(3, rows_of(a1n, h3), slot(ra2, h3), yp),
+        send(4, rows_of(b1n, h3), slot(rb2, h3), xp),
+        send(5, rows_of(a1, h3), slot(ra, h3), yp),
+        send(6, rows_of(b1, h3), slot(rb, h3), xp),
+        send(7, rows_of(a1, h3), rows_of(a1, h3), xp),
+        send(8, rows_of(b1, h3), rows_of(b1, h3), yp),
+        send(9, slot(ra, h3), rows_of(a1n, h3), xp),
+        send(10, slot(rb, h3), rows_of(b1n, h3), yp),
+        send(11, rows_of(own, h0), rows_of(own, h0), cp),
+    ]
+
+    def add(k, off, n, src):
+        sl = pl.ds(pl.multiple_of(off, 8), n)
+        acc[k, sl, :] = acc[k, sl, :] + src[k]
+
+    def loop(fn):
+        lax.fori_loop(0, n_chunk, lambda k, t: (fn(k), t)[1], 0)
+
+    for i, ld in enumerate(loads):
+        ld.wait()
+        cs[0](i).start()
+
+    def s1(k):
+        cs[0](k).wait_recv()
+        add(k, own, h0, r0)
+        cs[1](k).start()
+        cs[2](k).start()
+
+    def s2(k):
+        cs[1](k).wait()
+        add(k, a0, h2, ra)
+        cs[2](k).wait()
+        add(k, b0, h2, rb)
+        cs[3](k).start()
+        cs[4](k).start()
+
+    def g2(k):
+        cs[3](k).wait_recv()
+        add(k, a1, h3, ra2)
+        cs[4](k).wait_recv()
+        add(k, b1, h3, rb2)
+        for j in (5, 6, 7, 8):
+            cs[j](k).start()
+
+    def g1(k):
+        cs[5](k).wait_recv()
+        cs[9](k).start()
+        cs[6](k).wait_recv()
+        cs[10](k).start()
+        cs[3](k).wait_send()
+        acc[k, pl.ds(pl.multiple_of(a1n, 8), h3), :] = ra[k, 0:h3, :]
+        cs[4](k).wait_send()
+        acc[k, pl.ds(pl.multiple_of(b1n, 8), h3), :] = rb[k, 0:h3, :]
+
+    def g0(k):
+        for j in (7, 8, 9, 10):
+            cs[j](k).wait_recv()
+        cs[11](k).start()
+
+    loop(s1)
+    loop(s2)
+    loop(lambda k: cs[0](k).wait_send())
+    pl.semaphore_signal(free_sem, inc=1, device_id=(cp,), device_id_type=MESH)
+    loop(g2)
+    loop(g1)
+    pl.semaphore_wait(free_sem, 1)
+    loop(g0)
+    stores = [pltpu.make_async_copy(acc.at[i], dst, out_sem.at[i]) for i, dst in enumerate(outs)]
+    for i, st in enumerate(stores):
+        cs[11](i).wait_recv()
+        st.start()
+
+    def finish(k):
+        for j in range(5, 12):
+            cs[j](k).wait_send()
+
+    loop(finish)
+    for st in stores:
+        st.wait()
+
+
+def all_reduce(grads):
+    dm, ff = grads[4].shape
+    n_chunk = 4 + 2 * (ff // dm)
+    anyspec = pl.BlockSpec(memory_space=pl.ANY)
+    return pl.pallas_call(
+        functools.partial(reduce_kernel, n_chunk),
+        out_shape=tuple(jax.ShapeDtypeStruct(g.shape, F32) for g in grads),
+        in_specs=[anyspec] * 6,
+        out_specs=[anyspec] * 6,
+        scratch_shapes=[
+            pltpu.VMEM((n_chunk, dm, dm), F32),
+            pltpu.VMEM((n_chunk, dm // 2, dm), F32),
+            pltpu.VMEM((n_chunk, dm // 8, dm), F32),
+            pltpu.VMEM((n_chunk, dm // 8, dm), F32),
+            pltpu.VMEM((n_chunk, dm // 16, dm), F32),
+            pltpu.VMEM((n_chunk, dm // 16, dm), F32),
+            pltpu.SemaphoreType.DMA((n_chunk,)),
+            pltpu.SemaphoreType.DMA((n_chunk,)),
+            pltpu.SemaphoreType.DMA((12, n_chunk)),
+            pltpu.SemaphoreType.DMA((12, n_chunk)),
+            pltpu.SemaphoreType.REGULAR,
+        ],
+        compiler_params=pltpu.CompilerParams(collective_id=0, has_side_effects=True, vmem_limit_bytes=40 * 2 ** 20),
+    )(*grads)
 
 
 def solution(mesh):
@@ -243,7 +407,7 @@
             compiler_params=pltpu.CompilerParams(vmem_limit_bytes=67043328),
         )(x_loc.reshape(tok, dm), g_loc.reshape(tok, dm), step_emb.astype(F32)[:, None, :],
           *wts, w_o.reshape(n_heads * hd, dm), w_up, w_down)
-        sums = lax.psum(tuple(outs[:6]), 'data')
+        sums = all_reduce(tuple(outs[:6]))
         heads = [a.reshape(n_heads, hd, dm).transpose(2, 0, 1) for a in sums[:3]]
         return (*heads, sums[3].reshape(n_heads, hd, dm), sums[4], sums[5], outs[6].reshape(n_seq, seq, dm))
 

time: 223 us -> 179 us (0.80)
  waiting for transfers between devices: 104 us -> 0 us
  Pallas kernels: 93.4 us -> 163 us
  between operations: 14 us -> 0.65 us
  local copies, waits for them, and re-layouts: 10.8 us -> 14.9 us
    psum x1 -> x0, waiting for transfers between devices: 104 us -> none  [per_device(): sums = lax.psum(tuple(outs[:6]), 'data')]
    pallas_call x0 -> x1, Pallas kernels: none -> 69.3 us  [all_reduce(): pl.pallas_call(functools.partial(reduce_kernel, n_chunk), out_shape=tuple...]
    unnamed x14 -> x18, local copies, waits for them, and re-layouts: 9.54 us -> 13.7 us
  transfers between devices with their start and end apart: 1 -> 0, of which waited for: 1 -> 0; matrix products, arithmetic and copies ran while one was open for 0% -> 0% of each run, Pallas kernels for 0% -> 0%
where the time goes in v1:
time: 179 us; the launch traced here: 178 us
  Pallas kernels  163 us (91%)
  local copies, waits for them, and re-layouts  14.9 us (8%)
    pallas_call x1, Pallas kernels, per_device(): pl.pallas_call(functools.partial(block_kernel, n_seq, seq, n_layers, n_he...  93.4 us
    pallas_call x1, Pallas kernels, all_reduce(): pl.pallas_call(functools.partial(reduce_kernel, n_chunk), out_shape=tuple...  69.3 us
    unnamed x18, local copies, waits for them, and re-layouts  13.7 us

profile of v1, /device:TPU:0, one launch (start us, length us, event | category | flops | bytes accessed | tf_op | source)
XLA Modules:
  0.0 178.3 jit_solution(7058516050880633920)
XLA Ops:
  0.6 1.3 reshape.58.emb_ref
  1.9 93.4 %shard_map.144 = (f32[384,384]{1,0:T(8,128)}, f32[384,384]{1,0:T(8,128)}, f32[384,384]{1,0:T(8,128)}, f32[384,384]{1,0:T(8,128)}, f32[384,1536]{1,0:T(8,128)}, /...) custom-call(bf16[512,384]{1,0:T(8,128)(2,1)} %bitcast.27, bf16[512,384]{1,0:T(8,128)(2,1)} %bitcast.28, ...), custom_call_target="tpu_custom_call" | custom-call | tf_op jit(solution)/shard_map/pallas_call | solution.py:380
  95.3 0.0 copy-start
  95.3 1.7 copy-done
  97.0 0.0 copy-start.1
  97.0 1.7 copy-done.1
  98.6 0.0 copy-start.2
  98.6 1.1 copy-done.2
  99.7 0.0 copy-start.3
  99.7 1.1 copy-done.3
  100.8 0.0 copy-start.4
  100.8 1.1 copy-done.4
  101.8 0.0 copy-start.5
  101.8 1.1 copy-done.5
  102.9 69.3 %shard_map.145 = (f32[384,384]{1,0:T(8,128)S(1)}, f32[384,384]{1,0:T(8,128)S(1)}, f32[384,384]{1,0:T(8,128)S(1)}, f32[384,384]{1,0:T(8,128)S(1)}, f32[384,1536]{1,0:T(8,128)S(1)}, /*index=5*/f32[1536,384]{1,0:T(8,128)S(1)}) custom-call(f32[384,384]{1,0:T(8,128)S(1)} %copy-done.2, f32[384,384]{1,0:T(8,128)S(1)} %copy-done.3, f32[384,384]{1,0:T(8,128)S(1)} %copy-done.4, ...), custom_call_target="tpu_custom_call" | custom-call | tf_op jit(solution)/shard_map/pallas_call | solution.py:345
  172.2 0.8 copy.22
  173.0 0.8 copy.23
  173.9 0.8 copy.24
  174.7 0.8 copy.25
  175.5 1.4 copy.26
  176.9 1.4 copy.27
Async XLA Ops:
  95.3 1.7 copy-start
  97.0 1.7 copy-start.1
  98.6 1.1 copy-start.2
  99.7 1.1 copy-start.3
  100.8 1.1 copy-start.4
  101.8 1.1 copy-start.5

commit v2 on v1

v2 whole, which is shorter than its diff:
```python
import functools
import math

import jax
import jax.numpy as jnp
from jax import lax
from jax.experimental import pallas as pl
from jax.experimental.pallas import tpu as pltpu
from jax.sharding import PartitionSpec as P

EPS = 1e-6
F32 = jnp.float32
BF16 = jnp.bfloat16
MESH = pl.DeviceIdType.MESH
LOG2E = math.log2(math.e)
GC0 = math.sqrt(2.0 / math.pi)
GC1 = GC0 * 0.044715
NT = (((1,), (1,)), ((), ()))
TN = (((0,), (0,)), ((), ()))
VMEM_LIMIT = 58851328


def mm(a, b):
    return jnp.dot(a, b, preferred_element_type=F32)


def mmg(a, b, dims):
    return lax.dot_general(a, b, dims, preferred_element_type=F32)


def blocks(total, size):
    return [(s, min(size, total - s)) for s in range(0, total, size)]


def rms_scale(xf):
    return lax.rsqrt(jnp.mean(xf * xf, axis=-1, keepdims=True) + EPS)


def norm_back(xf, r, dy):
    inner = jnp.mean(xf * dy, axis=-1, keepdims=True)
    return dy * r - xf * (r * r * r * inner)


def block_kernel(n_seq, seq, n_layers, n_heads,
                 x_hbm, g_hbm, emb_ref, wq_hbm, wk_hbm, wv_hbm, wo_hbm, wup_hbm, wdn_hbm,
                 acc, dx_ref,
                 wqkv_s, wqkvt_s, wo_s, wot_s, wup_s, wupt_s, wdn_s, wdnt_s, emb_s,
                 x_s, qkv_s, p_s, mix_s, h_s, z_s,
                 u_s, g_s, dup_s, dn_s, dqkv_s, d_s, dmid_s, st_s,
                 r0, ra, rb, ra2, rb2, in_sem, ssem, rsem, free_sem):
    tok, dm = d_s.shape
    ff = wup_s.shape[1]
    hd = dm // n_heads
    pw = 2 * hd
    n_pair = n_heads // 2
    n_dn = ff // dm
    n_chunk = 2 * n_dn + 4
    k_o, k_q = 2 * n_dn, 2 * n_dn + 1
    scale = hd ** -0.5
    NB = 256
    rows = blocks(tok, 64)
    rows_b = blocks(tok, 32)

    me = lax.axis_index('data')
    c = lax.rem(me, 2)
    x = lax.rem(lax.div(me, 2), 2)
    y = lax.div(me, 4)
    cp = me + 1 - 2 * c
    xp = me + 2 - 4 * x
    yp = me + 4 - 8 * y
    barrier = pltpu.get_barrier_semaphore()
    for p in (cp, xp, yp):
        pl.semaphore_signal(barrier, inc=1, device_id=(p,), device_id_type=MESH)

    loads = [pltpu.make_async_copy(src, dst, in_sem.at[i]) for i, (src, dst) in enumerate((
        (wq_hbm, wqkvt_s.at[0:dm, :]), (wk_hbm, wqkvt_s.at[dm:2 * dm, :]), (wv_hbm, wqkvt_s.at[2 * dm:3 * dm, :]),
        (x_hbm, d_s), (wo_hbm, wo_s), (wup_hbm, wup_s), (wdn_hbm, wdn_s), (g_hbm, dmid_s)))]
    for ld in loads:
        ld.start()
    emb = emb_ref[...].astype(F32)
    for l in range(n_layers):
        emb_s[l] = emb[l:l + 1]
    acc[...] = jnp.zeros(acc.shape, F32)
    for i in range(3):
        loads[i].wait()
        wqkv_s[:, i * dm:(i + 1) * dm] = wqkvt_s[i * dm:(i + 1) * dm, :].T
    for ld in loads[3:]:
        ld.wait()
    wot_s[...] = wo_s[...].T
    wupt_s[...] = wup_s[...].T
    wdnt_s[...] = wdn_s[...].T

    low = lax.broadcasted_iota(jnp.int32, (seq, pw), 1) < hd

    def stack(a):
        zero = jnp.zeros_like(a)
        return jnp.concatenate([jnp.where(low, a, zero), jnp.where(low, zero, a)], axis=0)

    def halves(a):
        return a[:seq], a[seq:]

    def beside(a):
        return jnp.concatenate(halves(a), axis=1)

    def seq_rows(s):
        return slice(s * seq, (s + 1) * seq)

    def fwd(l, carry):
        emb_l = emb_s[l]
        for r_0, rn in rows:
            rs = slice(r_0, r_0 + rn)
            xb = (d_s[rs, :].astype(F32) + emb_l).astype(BF16)
            x_s[l, rs, :] = xb
            xf = xb.astype(F32)
            u_s[rs, :] = (xf * rms_scale(xf)).astype(BF16)
        for n0, nn in blocks(3 * dm, NB):
            ns = slice(n0, n0 + nn)
            qkv_s[l, :, ns] = mm(u_s[...], wqkv_s[:, ns]).astype(BF16)

        def scores(s):
            rs = seq_rows(s)
            for j in range(n_pair):
                cc = j * pw
                k = stack(qkv_s[l, rs, dm + cc:dm + cc + pw])
                st_s[s * n_pair + j] = mmg(k, qkv_s[l, rs, cc:cc + pw], NT).astype(BF16)

        def soft(s):
            for j in range(n_pair):
                for i, half in enumerate(halves(st_s[s * n_pair + j])):
                    sf = half.astype(F32)
                    top = jnp.max(sf, axis=0, keepdims=True)
                    e = jnp.exp2((sf - top) * (scale * LOG2E))
                    pr = e * (1.0 / jnp.sum(e, axis=0, keepdims=True))
                    p_s[l, s * n_pair + j, i * seq:(i + 1) * seq, :] = pr

        def mix(s):
            rs = seq_rows(s)
            for j in range(n_pair):
                cc = j * pw
                v = stack(qkv_s[l, rs, 2 * dm + cc:2 * dm + cc + pw])
                pb = p_s[l, s * n_pair + j].astype(BF16)
                mix_s[l, rs, cc:cc + pw] = mmg(pb, v, TN).astype(BF16)

        for s in range(n_seq + 2):
            if s < n_seq:
                scores(s)
            if 1 <= s <= n_seq:
                soft(s - 1)
            if s >= 2:
                mix(s - 2)
        for n0, nn in blocks(dm, NB):
            ns = slice(n0, n0 + nn)
            o = mm(mix_s[l], wo_s[:, ns]).astype(BF16)
            h_s[l, :, ns] = (x_s[l, :, ns].astype(F32) + o.astype(F32)).astype(BF16)
        for r_0, rn in rows:
            rs = slice(r_0, r_0 + rn)
            hf = h_s[l, rs, :].astype(F32)
            u_s[rs, :] = (hf * rms_scale(hf)).astype(BF16)
        for n0, nn in blocks(ff, NB):
            ns = slice(n0, n0 + nn)
            zb = mm(u_s[...], wup_s[:, ns]).astype(BF16)
            z_s[l, :, ns] = zb
            for r_0, rn in rows:
                z = zb[r_0:r_0 + rn].astype(F32)
                cdf = 0.5 + 0.5 * jnp.tanh(z * (GC0 + GC1 * (z * z)))
                g_s[r_0:r_0 + rn, ns] = (z * cdf).astype(BF16)
        for n0, nn in blocks(dm, NB):
            ns = slice(n0, n0 + nn)
            yd = mm(g_s[...], wdn_s[:, ns]).astype(BF16)
            d_s[:, ns] = (h_s[l, :, ns].astype(F32) + yd.astype(F32)).astype(BF16)
        return carry

    lax.fori_loop(0, n_layers, fwd, 0)
    d_s[...] = dmid_s[...]

    def bwd(l, hook):
        fb = blocks(ff, NB)

        def dact(i):
            n0, nn = fb[i]
            ns = slice(n0, n0 + nn)
            dup_s[:, ns] = mm(d_s[...], wdnt_s[:, ns]).astype(BF16)

        def gelu_back(i):
            n0, nn = fb[i]
            ns = slice(n0, n0 + nn)
            for r_0, rn in rows_b:
                rs = slice(r_0, r_0 + rn)
                z = z_s[l, rs, ns].astype(F32)
                z2 = z * z
                cdf = 0.5 + 0.5 * jnp.tanh(z * (GC0 + GC1 * z2))
                g = z * cdf
                g_s[rs, ns] = g.astype(BF16)
                dg = cdf + (g * (1.0 - cdf)) * (2.0 * GC0 + 6.0 * GC1 * z2)
                dup_s[rs, ns] = (dup_s[rs, ns].astype(F32) * dg).astype(BF16)

        def wg_down(i):
            n0, nn = fb[i]
            res = mmg(g_s[:, n0:n0 + nn], d_s[...], TN)
            for t in range(0, nn, 128):
                r = n0 + t
                acc[r // dm, r % dm:r % dm + 128, :] += res[t:t + 128]

        def wg_up(i):
            n0, nn = fb[i]
            res = mmg(u_s[...], dup_s[:, n0:n0 + nn], TN)
            for t in range(0, nn, 128):
                r = n0 + t
                acc[n_dn + r // dm, :, r % dm:r % dm + 128] += res[:, t:t + 128]

        def wg_qkv(i):
            acc[k_q + i] += mmg(dqkv_s[:, i * dm:(i + 1) * dm], u_s[...], TN)

        dact(0)
        for r_0, rn in rows:
            rs = slice(r_0, r_0 + rn)
            hf = h_s[l, rs, :].astype(F32)
            u_s[rs, :] = (hf * rms_scale(hf)).astype(BF16)
        for i in range(len(fb)):
            if i + 1 < len(fb):
                dact(i + 1)
            gelu_back(i)
            if i >= 1:
                wg_down(i - 1)
        wg_down(len(fb) - 1)
        hook(0)
        for n0, nn in blocks(dm, NB):
            ns = slice(n0, n0 + nn)
            dn_s[:, ns] = mm(dup_s[...], wupt_s[:, ns]).astype(BF16)
        for i, (r_0, rn) in enumerate(rows_b):
            rs = slice(r_0, r_0 + rn)
            hf = h_s[l, rs, :].astype(F32)
            dh = norm_back(hf, rms_scale(hf), dn_s[rs, :].astype(F32)).astype(BF16)
            dmid_s[rs, :] = (d_s[rs, :].astype(F32) + dh.astype(F32)).astype(BF16)
            if i % 4 == 3 and i // 4 < 2:
                wg_up(i // 4)
        hook(1)
        for n0, nn in blocks(dm, NB):
            ns = slice(n0, n0 + nn)
            dn_s[:, ns] = mm(dmid_s[...], wot_s[:, ns]).astype(BF16)

        def dprob(s):
            rs = seq_rows(s)
            for j in range(n_pair):
                cc = j * pw
                v = stack(qkv_s[l, rs, 2 * dm + cc:2 * dm + cc + pw])
                st_s[s * n_pair + j] = mmg(v, dn_s[rs, cc:cc + pw], NT).astype(BF16)

        def dscore(s):
            for j in range(n_pair):
                i = s * n_pair + j
                for hh in range(2):
                    hs = slice(hh * seq, (hh + 1) * seq)
                    pf = p_s[l, i, hs, :]
                    dp = st_s[i, hs, :].astype(F32)
                    inner = jnp.sum(pf * dp, axis=0, keepdims=True)
                    st_s[i, hs, :] = (pf * (dp - inner) * scale).astype(BF16)

        def dqkv(s):
            rs = seq_rows(s)
            for j in range(n_pair):
                i = s * n_pair + j
                cc = j * pw
                dst = st_s[i]
                q = stack(qkv_s[l, rs, cc:cc + pw])
                k = stack(qkv_s[l, rs, dm + cc:dm + cc + pw])
                dmx = stack(dn_s[rs, cc:cc + pw])
                dqkv_s[rs, cc:cc + pw] = mmg(dst, k, TN).astype(BF16)
                dqkv_s[rs, dm + cc:dm + cc + pw] = mm(beside(dst), q).astype(BF16)
                pb = p_s[l, i].astype(BF16)
                dqkv_s[rs, 2 * dm + cc:2 * dm + cc + pw] = mm(beside(pb), dmx).astype(BF16)

        for s in range(n_seq + 2):
            if s < n_seq:
                dprob(s)
                wg_up(2 + s)
            if 1 <= s <= n_seq:
                dscore(s - 1)
            if s == 2:
                acc[k_o] += mmg(mix_s[l], dmid_s[...], TN)
            if s >= 2:
                dqkv(s - 2)
            if s == n_seq - 1:
                hook(2)
        hook(3)
        for r_0, rn in rows:
            rs = slice(r_0, r_0 + rn)
            xf = x_s[l, rs, :].astype(F32)
            u_s[rs, :] = (xf * rms_scale(xf)).astype(BF16)
        for n0, nn in blocks(dm, NB):
            ns = slice(n0, n0 + nn)
            dn_s[:, ns] = mm(dqkv_s[...], wqkvt_s[:, ns]).astype(BF16)
        for i, (r_0, rn) in enumerate(rows_b):
            rs = slice(r_0, r_0 + rn)
            xf = x_s[l, rs, :].astype(F32)
            dh = norm_back(xf, rms_scale(xf), dn_s[rs, :].astype(F32)).astype(BF16)
            d_s[rs, :] = (dmid_s[rs, :].astype(F32) + dh.astype(F32)).astype(BF16)
            if i % 4 == 3 and i // 4 < 3:
                wg_qkv(i // 4)
        hook(4)

    def bwd_body(i, carry):
        bwd(n_layers - 1 - i, lambda n: None)
        return carry

    lax.fori_loop(0, n_layers - 1, bwd_body, 0)
    pl.semaphore_wait(barrier, 3)

    h0, h1, h2, h3 = dm // 2, dm // 4, dm // 8, dm // 16
    own = c * h0
    oth = (1 - c) * h0
    a0, a0n = own + x * h2, own + (1 - x) * h2
    b0, b0n = own + h1 + y * h2, own + h1 + (1 - y) * h2
    a1, a1n = a0 + y * h3, a0 + (1 - y) * h3
    b1, b1n = b0 + x * h3, b0 + (1 - x) * h3

    def part(k, off, n):
        return acc.at[k, pl.ds(pl.multiple_of(off, 8), n), :]

    def send(j, src, dst, dev):
        def at(k):
            return pltpu.make_async_remote_copy(
                src_ref=src(k), dst_ref=dst(k), send_sem=ssem.at[j, k], recv_sem=rsem.at[j, k],
                device_id=(dev,), device_id_type=MESH)
        return at

    def rows_of(off, n):
        return lambda k: part(k, off, n)

    def slot(ref, n):
        return lambda k: ref.at[k, 0:n, :]

    cs = [
        send(0, rows_of(oth, h0), slot(r0, h0), cp),
        send(1, rows_of(a0n, h2), slot(ra, h2), xp),
        send(2, rows_of(b0n, h2), slot(rb, h2), yp),
        send(3, rows_of(a1n, h3), slot(ra2, h3), yp),
        send(4, rows_of(b1n, h3), slot(rb2, h3), xp),
        send(5, rows_of(a1, h3), slot(ra, h3), yp),
        send(6, rows_of(b1, h3), slot(rb, h3), xp),
        send(7, rows_of(a1, h3), rows_of(a1, h3), xp),
        send(8, rows_of(b1, h3), rows_of(b1, h3), yp),
        send(9, slot(ra, h3), rows_of(a1n, h3), xp),
        send(10, slot(rb, h3), rows_of(b1n, h3), yp),
        send(11, rows_of(own, h0), rows_of(own, h0), cp),
    ]

    def add(k, off, n, src):
        sl = pl.ds(pl.multiple_of(off, 8), n)
        acc[k, sl, :] = acc[k, sl, :] + src[k]

    def loop(fn, lo=0, hi=n_chunk):
        lax.fori_loop(lo, hi, lambda k, t: (fn(k), t)[1], 0)

    def s0(k):
        cs[0](k).start()

    def s1(k):
        cs[0](k).wait_recv()
        add(k, own, h0, r0)
        cs[1](k).start()
        cs[2](k).start()

    def s2(k):
        cs[1](k).wait()
        add(k, a0, h2, ra)
        cs[2](k).wait()
        add(k, b0, h2, rb)
        cs[3](k).start()
        cs[4](k).start()

    def g2(k):
        cs[3](k).wait_recv()
        add(k, a1, h3, ra2)
        cs[4](k).wait_recv()
        add(k, b1, h3, rb2)
        for j in (5, 6, 7, 8):
            cs[j](k).start()

    def g1(k):
        cs[5](k).wait_recv()
        cs[9](k).start()
        cs[6](k).wait_recv()
        cs[10](k).start()
        cs[3](k).wait_send()
        acc[k, pl.ds(pl.multiple_of(a1n, 8), h3), :] = ra[k, 0:h3, :]
        cs[4](k).wait_send()
        acc[k, pl.ds(pl.multiple_of(b1n, 8), h3), :] = rb[k, 0:h3, :]

    def g0(k):
        for j in (7, 8, 9, 10):
            cs[j](k).wait_recv()
        cs[11](k).start()

    def finish(k):
        cs[11](k).wait_recv()
        for j in range(5, 12):
            cs[j](k).wait_send()

    def hook(n):
        if n == 0:
            loop(s0, 0, n_dn)
        elif n == 1:
            loop(s1, 0, n_dn)
        elif n == 2:
            loop(s0, n_dn, k_o + 1)
        elif n == 3:
            loop(s1, n_dn, k_o + 1)
        elif n == 4:
            loop(s0, k_q, n_chunk)

    bwd(0, hook)
    dx_ref[...] = d_s[...]
    loop(s1, k_q, n_chunk)
    loop(s2)
    loop(lambda k: cs[0](k).wait_send())
    pl.semaphore_signal(free_sem, inc=1, device_id=(cp,), device_id_type=MESH)
    loop(g2)
    loop(g1)
    pl.semaphore_wait(free_sem, 1)
    loop(g0)
    loop(finish)


def store_kernel(acc, dx_ref, oq, ok, ov, oo, oup, odn, odx, sem):
    dm = acc.shape[1]
    n = odn.shape[0] // dm
    dst = ([odn.at[i * dm:(i + 1) * dm, :] for i in range(n)]
           + [oup.at[:, i * dm:(i + 1) * dm] for i in range(n)] + [oo, oq, ok, ov])
    cps = [pltpu.make_async_copy(acc.at[i], d, sem.at[i]) for i, d in enumerate(dst)]
    cps.append(pltpu.make_async_copy(dx_ref, odx, sem.at[len(dst)]))
    for cc in cps:
        cc.start()
    for cc in cps:
        cc.wait()


def solution(mesh):
    batch_spec = P('data', None, None)

    def per_device(x_loc, g_loc, step_emb, w_q, w_k, w_v, w_o, w_up, w_down):
        n_seq, seq, dm = x_loc.shape
        n_layers = step_emb.shape[0]
        n_heads, hd = w_q.shape[1:]
        ff = w_up.shape[1]
        tok = n_seq * seq
        n_pair = n_heads // 2
        n_chunk = 4 + 2 * (ff // dm)
        wts = [w.transpose(1, 2, 0).reshape(n_heads * hd, dm) for w in (w_q, w_k, w_v)]
        vm = pl.BlockSpec(memory_space=pltpu.VMEM)
        hb = pl.BlockSpec(memory_space=pl.ANY)
        acc, dx = pl.pallas_call(
            functools.partial(block_kernel, n_seq, seq, n_layers, n_heads),
            out_shape=(pltpu.VMEM((n_chunk, dm, dm), F32), pltpu.VMEM((tok, dm), BF16)),
            in_specs=[hb, hb, vm] + [hb] * 6,
            out_specs=[vm] * 2,
            scratch_shapes=[
                pltpu.VMEM((dm, 3 * dm), BF16),
                pltpu.VMEM((3 * dm, dm), BF16),
                pltpu.VMEM((dm, dm), BF16),
                pltpu.VMEM((dm, dm), BF16),
                pltpu.VMEM((dm, ff), BF16),
                pltpu.VMEM((ff, dm), BF16),
                pltpu.VMEM((ff, dm), BF16),
                pltpu.VMEM((dm, ff), BF16),
                pltpu.VMEM((n_layers, 1, dm), F32),
                pltpu.VMEM((n_layers, tok, dm), BF16),
                pltpu.VMEM((n_layers, tok, 3 * dm), BF16),
                pltpu.VMEM((n_layers, n_seq * n_pair, 2 * seq, seq), F32),
                pltpu.VMEM((n_layers, tok, dm), BF16),
                pltpu.VMEM((n_layers, tok, dm), BF16),
                pltpu.VMEM((n_layers, tok, ff), BF16),
                pltpu.VMEM((tok, dm), BF16),
                pltpu.VMEM((tok, ff), BF16),
                pltpu.VMEM((tok, ff), BF16),
                pltpu.VMEM((tok, dm), BF16),
                pltpu.VMEM((tok, 3 * dm), BF16),
                pltpu.VMEM((tok, dm), BF16),
                pltpu.VMEM((tok, dm), BF16),
                pltpu.VMEM((n_seq * n_pair, 2 * seq, seq), BF16),
                pltpu.VMEM((n_chunk, dm // 2, dm), F32),
                pltpu.VMEM((n_chunk, dm // 8, dm), F32),
                pltpu.VMEM((n_chunk, dm // 8, dm), F32),
                pltpu.VMEM((n_chunk, dm // 16, dm), F32),
                pltpu.VMEM((n_chunk, dm // 16, dm), F32),
                pltpu.SemaphoreType.DMA((8,)),
                pltpu.SemaphoreType.DMA((12, n_chunk)),
                pltpu.SemaphoreType.DMA((12, n_chunk)),
                pltpu.SemaphoreType.REGULAR,
            ],
            compiler_params=pltpu.CompilerParams(
                collective_id=0, has_side_effects=True, vmem_limit_bytes=VMEM_LIMIT),
        )(x_loc.reshape(tok, dm), g_loc.reshape(tok, dm), step_emb,
          *wts, w_o.reshape(n_heads * hd, dm), w_up, w_down)
        sq = jax.ShapeDtypeStruct((dm, dm), F32)
        gq, gk, gv, go, gup, gdn, gx = pl.pallas_call(
            store_kernel,
            out_shape=(sq, sq, sq, sq, jax.ShapeDtypeStruct((dm, ff), F32), jax.ShapeDtypeStruct((ff, dm), F32),
                       jax.ShapeDtypeStruct((tok, dm), BF16)),
            in_specs=[vm] * 2,
            out_specs=[hb] * 7,
            scratch_shapes=[pltpu.SemaphoreType.DMA((n_chunk + 1,))],
            compiler_params=pltpu.CompilerParams(vmem_limit_bytes=2 ** 20),
        )(acc, dx)
        heads = [a.reshape(n_heads, hd, dm).transpose(2, 0, 1) for a in (gq, gk, gv)]
        return (*heads, go.reshape(n_heads, hd, dm), gup, gdn, gx.reshape(n_seq, seq, dm))

    return jax.shard_map(per_device, mesh=mesh, in_specs=(batch_spec, batch_spec, P(), P(), P(), P(), P(), P(), P()), out_specs=(P(), P(), P(), P(), P(), P(), batch_spec), check_vma=False)
```

time: 179 us -> 141 us (0.79)
  Pallas kernels: 163 us -> 140 us
  local copies, waits for them, and re-layouts: 14.9 us -> 0 us
    pallas_call x1, Pallas kernels: 69.3 us -> 3.12 us  [per_device(): pl.pallas_call(store_kernel, out_shape=(sq, sq, sq, sq, jax.ShapeDtypeStr...]
    pallas_call x1, Pallas kernels: 93.4 us -> 137 us  [per_device(): pl.pallas_call(functools.partial(block_kernel, n_seq, seq, n_layers, n_he...]
    unnamed x18 -> x0, local copies, waits for them, and re-layouts: 13.7 us -> none
where the time goes in v2:
time: 141 us
  Pallas kernels  140 us (99%)
    pallas_call x1, Pallas kernels, per_device(): pl.pallas_call(functools.partial(block_kernel, n_seq, seq, n_layers, n_he...  137 us
    pallas_call x1, Pallas kernels, per_device(): pl.pallas_call(store_kernel, out_shape=(sq, sq, sq, sq, jax.ShapeDtypeStr...  3.12 us

profile of v2, /device:TPU:0, one launch (start us, length us, event | category | flops | bytes accessed | tf_op | source)
XLA Modules:
  0.0 140.7 jit_solution(5867865496976440087)
XLA Ops:
  0.6 136.7 %shard_map.144 = (f32[12,384,384]{2,1,0:T(8,128)S(1)}, bf16[512,384]{1,0:T(8,128)(2,1)S(1)}) custom-call(bf16[512,384]{1,0:T(8,128)(2,1)} %bitcast.23, bf16[512,384]{1,0:T(8,128)(2,1)} %bitcast.24, bf16[6,384]{1,0:T(8,128)(2,1)} %emb_ref.1, bf16[384,384]{1,0:T(8,128)(2,1)} %bitcast.25, bf16[384,384]{1,0:T(8,128)(2,1)} %bitcast.26, ...), custom_call_target="tpu_custom_call" | custom-call | tf_op jit(solution)/shard_map/pallas_call | solution.py:452
  137.4 3.1 %shard_map.145 = (f32[384,384]{1,0:T(8,128)}, f32[384,384]{1,0:T(8,128)}, f32[384,384]{1,0:T(8,128)}, f32[384,384]{1,0:T(8,128)}, f32[384,1536]{1,0:T(8,128)}, /...) custom-call(f32[12,384,384]{2,1,0:T(8,128)S(1)} %get-tuple-element.16.acc, bf16[512,384]{1,0:T(8,128)(2,1)S(1)} %get-tuple-element.17.dx_ref), custom_call_target="tpu_custom_call" | custom-call | tf_op jit(solution)/shard_map/pallas_call | solution.py:496

commit v3 on v2

--- a/solution.py
+++ b/solution.py
@@ -18,6 +18,7 @@
 NT = (((1,), (1,)), ((), ()))
 TN = (((0,), (0,)), ((), ()))
 VMEM_LIMIT = 58851328
+BLOCK = 256
 
 
 def mm(a, b):
@@ -46,10 +47,11 @@
                  acc, dx_ref,
                  wqkv_s, wqkvt_s, wo_s, wot_s, wup_s, wupt_s, wdn_s, wdnt_s, emb_s,
                  x_s, qkv_s, p_s, mix_s, h_s, z_s,
-                 u_s, g_s, dup_s, dn_s, dqkv_s, d_s, dmid_s, st_s,
+                 u_s, g_s, da_s, yp_s, dn_s, d_s, dmid_s, st_s,
                  r0, ra, rb, ra2, rb2, in_sem, ssem, rsem, free_sem):
     tok, dm = d_s.shape
     ff = wup_s.shape[1]
+    fb = blocks(ff, BLOCK)
     hd = dm // n_heads
     pw = 2 * hd
     n_pair = n_heads // 2
@@ -57,7 +59,7 @@
     n_chunk = 2 * n_dn + 4
     k_o, k_q = 2 * n_dn, 2 * n_dn + 1
     scale = hd ** -0.5
-    NB = 256
+    NB = BLOCK
     rows = blocks(tok, 64)
     rows_b = blocks(tok, 32)
 
@@ -74,21 +76,19 @@
 
     loads = [pltpu.make_async_copy(src, dst, in_sem.at[i]) for i, (src, dst) in enumerate((
         (wq_hbm, wqkvt_s.at[0:dm, :]), (wk_hbm, wqkvt_s.at[dm:2 * dm, :]), (wv_hbm, wqkvt_s.at[2 * dm:3 * dm, :]),
-        (x_hbm, d_s), (wo_hbm, wo_s), (wup_hbm, wup_s), (wdn_hbm, wdn_s), (g_hbm, dmid_s)))]
+        (x_hbm, d_s), (wo_hbm, wo_s), (wup_hbm, wup_s), (wdn_hbm, wdn_s), (g_hbm, dmid_s.at[0])))]
     for ld in loads:
         ld.start()
     emb = emb_ref[...].astype(F32)
     for l in range(n_layers):
         emb_s[l] = emb[l:l + 1]
-    acc[...] = jnp.zeros(acc.shape, F32)
+    acc[0:n_dn] = jnp.zeros((n_dn, dm, dm), F32)
     for i in range(3):
         loads[i].wait()
         wqkv_s[:, i * dm:(i + 1) * dm] = wqkvt_s[i * dm:(i + 1) * dm, :].T
     for ld in loads[3:]:
         ld.wait()
     wot_s[...] = wo_s[...].T
-    wupt_s[...] = wup_s[...].T
-    wdnt_s[...] = wdn_s[...].T
 
     low = lax.broadcasted_iota(jnp.int32, (seq, pw), 1) < hd
 
@@ -107,6 +107,10 @@
 
     def fwd(l, carry):
         emb_l = emb_s[l]
+        tl = ff // n_layers
+        ts = pl.ds(pl.multiple_of(l * tl, tl), tl)
+        wupt_s[ts, :] = wup_s[:, ts].T
+        wdnt_s[:, ts] = wdn_s[ts, :].T
         for r_0, rn in rows:
             rs = slice(r_0, r_0 + rn)
             xb = (d_s[rs, :].astype(F32) + emb_l).astype(BF16)
@@ -156,30 +160,43 @@
             rs = slice(r_0, r_0 + rn)
             hf = h_s[l, rs, :].astype(F32)
             u_s[rs, :] = (hf * rms_scale(hf)).astype(BF16)
-        for n0, nn in blocks(ff, NB):
-            ns = slice(n0, n0 + nn)
-            zb = mm(u_s[...], wup_s[:, ns]).astype(BF16)
-            z_s[l, :, ns] = zb
+        def up(i):
+            n0, nn = fb[i]
+            ns = slice(n0, n0 + nn)
+            z_s[l, :, ns] = mm(u_s[...], wup_s[:, ns]).astype(BF16)
+
+        def gelu(i):
+            n0, nn = fb[i]
+            ns = slice(n0, n0 + nn)
             for r_0, rn in rows:
-                z = zb[r_0:r_0 + rn].astype(F32)
+                rs = slice(r_0, r_0 + rn)
+                z = z_s[l, rs, ns].astype(F32)
                 cdf = 0.5 + 0.5 * jnp.tanh(z * (GC0 + GC1 * (z * z)))
-                g_s[r_0:r_0 + rn, ns] = (z * cdf).astype(BF16)
+                g_s[rs, ns] = (z * cdf).astype(BF16)
+
+        half = len(fb) // 2 * BLOCK
+        up(0)
+        for i in range(len(fb)):
+            if i + 1 < len(fb):
+                up(i + 1)
+            gelu(i)
+            if i + 1 == len(fb) - 1:
+                for n0, nn in blocks(dm, NB):
+                    ns = slice(n0, n0 + nn)
+                    yp_s[:, ns] = mm(g_s[:, :half], wdn_s[:half, ns])
         for n0, nn in blocks(dm, NB):
             ns = slice(n0, n0 + nn)
-            yd = mm(g_s[...], wdn_s[:, ns]).astype(BF16)
+            yd = (yp_s[:, ns] + mm(g_s[:, half:], wdn_s[half:, ns])).astype(BF16)
             d_s[:, ns] = (h_s[l, :, ns].astype(F32) + yd.astype(F32)).astype(BF16)
         return carry
 
     lax.fori_loop(0, n_layers, fwd, 0)
-    d_s[...] = dmid_s[...]
-
-    def bwd(l, hook):
-        fb = blocks(ff, NB)
-
+    d_s[...] = dmid_s[0]
+
+    def gelu_phase(l, after):
         def dact(i):
             n0, nn = fb[i]
-            ns = slice(n0, n0 + nn)
-            dup_s[:, ns] = mm(d_s[...], wdnt_s[:, ns]).astype(BF16)
+            da_s[i % 2] = mm(d_s[...], wdnt_s[:, n0:n0 + nn]).astype(BF16)
 
         def gelu_back(i):
             n0, nn = fb[i]
@@ -192,7 +209,7 @@
                 g = z * cdf
                 g_s[rs, ns] = g.astype(BF16)
                 dg = cdf + (g * (1.0 - cdf)) * (2.0 * GC0 + 6.0 * GC1 * z2)
-                dup_s[rs, ns] = (dup_s[rs, ns].astype(F32) * dg).astype(BF16)
+                z_s[l, rs, ns] = (da_s[i % 2, rs, :].astype(F32) * dg).astype(BF16)
 
         def wg_down(i):
             n0, nn = fb[i]
@@ -201,43 +218,33 @@
                 r = n0 + t
                 acc[r // dm, r % dm:r % dm + 128, :] += res[t:t + 128]
 
-        def wg_up(i):
-            n0, nn = fb[i]
-            res = mmg(u_s[...], dup_s[:, n0:n0 + nn], TN)
-            for t in range(0, nn, 128):
-                r = n0 + t
-                acc[n_dn + r // dm, :, r % dm:r % dm + 128] += res[:, t:t + 128]
-
-        def wg_qkv(i):
-            acc[k_q + i] += mmg(dqkv_s[:, i * dm:(i + 1) * dm], u_s[...], TN)
-
         dact(0)
-        for r_0, rn in rows:
-            rs = slice(r_0, r_0 + rn)
-            hf = h_s[l, rs, :].astype(F32)
-            u_s[rs, :] = (hf * rms_scale(hf)).astype(BF16)
         for i in range(len(fb)):
             if i + 1 < len(fb):
                 dact(i + 1)
             gelu_back(i)
             if i >= 1:
                 wg_down(i - 1)
+                after(i - 1)
         wg_down(len(fb) - 1)
-        hook(0)
+        after(len(fb) - 1)
+
+    def mid_phase(l):
         for n0, nn in blocks(dm, NB):
             ns = slice(n0, n0 + nn)
-            dn_s[:, ns] = mm(dup_s[...], wupt_s[:, ns]).astype(BF16)
-        for i, (r_0, rn) in enumerate(rows_b):
+            dn_s[:, ns] = mm(z_s[l], wupt_s[:, ns]).astype(BF16)
+        for r_0, rn in rows_b:
             rs = slice(r_0, r_0 + rn)
             hf = h_s[l, rs, :].astype(F32)
-            dh = norm_back(hf, rms_scale(hf), dn_s[rs, :].astype(F32)).astype(BF16)
-            dmid_s[rs, :] = (d_s[rs, :].astype(F32) + dh.astype(F32)).astype(BF16)
-            if i % 4 == 3 and i // 4 < 2:
-                wg_up(i // 4)
-        hook(1)
+            r = rms_scale(hf)
+            dh = norm_back(hf, r, dn_s[rs, :].astype(F32)).astype(BF16)
+            h_s[l, rs, :] = (hf * r).astype(BF16)
+            dmid_s[l, rs, :] = (d_s[rs, :].astype(F32) + dh.astype(F32)).astype(BF16)
+
+    def attn_phase(l):
         for n0, nn in blocks(dm, NB):
             ns = slice(n0, n0 + nn)
-            dn_s[:, ns] = mm(dmid_s[...], wot_s[:, ns]).astype(BF16)
+            dn_s[:, ns] = mm(dmid_s[l], wot_s[:, ns]).astype(BF16)
 
         def dprob(s):
             rs = seq_rows(s)
@@ -265,42 +272,37 @@
                 q = stack(qkv_s[l, rs, cc:cc + pw])
                 k = stack(qkv_s[l, rs, dm + cc:dm + cc + pw])
                 dmx = stack(dn_s[rs, cc:cc + pw])
-                dqkv_s[rs, cc:cc + pw] = mmg(dst, k, TN).astype(BF16)
-                dqkv_s[rs, dm + cc:dm + cc + pw] = mm(beside(dst), q).astype(BF16)
+                qkv_s[l, rs, cc:cc + pw] = mmg(dst, k, TN).astype(BF16)
+                qkv_s[l, rs, dm + cc:dm + cc + pw] = mm(beside(dst), q).astype(BF16)
                 pb = p_s[l, i].astype(BF16)
-                dqkv_s[rs, 2 * dm + cc:2 * dm + cc + pw] = mm(beside(pb), dmx).astype(BF16)
+                qkv_s[l, rs, 2 * dm + cc:2 * dm + cc + pw] = mm(beside(pb), dmx).astype(BF16)
 
         for s in range(n_seq + 2):
             if s < n_seq:
                 dprob(s)
-                wg_up(2 + s)
             if 1 <= s <= n_seq:
                 dscore(s - 1)
-            if s == 2:
-                acc[k_o] += mmg(mix_s[l], dmid_s[...], TN)
             if s >= 2:
                 dqkv(s - 2)
-            if s == n_seq - 1:
-                hook(2)
-        hook(3)
-        for r_0, rn in rows:
+
+    def in_phase(l):
+        for n0, nn in blocks(dm, NB):
+            ns = slice(n0, n0 + nn)
+            dn_s[:, ns] = mm(qkv_s[l], wqkvt_s[:, ns]).astype(BF16)
+        for r_0, rn in rows_b:
             rs = slice(r_0, r_0 + rn)
             xf = x_s[l, rs, :].astype(F32)
-            u_s[rs, :] = (xf * rms_scale(xf)).astype(BF16)
-        for n0, nn in blocks(dm, NB):
-            ns = slice(n0, n0 + nn)
-            dn_s[:, ns] = mm(dqkv_s[...], wqkvt_s[:, ns]).astype(BF16)
-        for i, (r_0, rn) in enumerate(rows_b):
-            rs = slice(r_0, r_0 + rn)
-            xf = x_s[l, rs, :].astype(F32)
-            dh = norm_back(xf, rms_scale(xf), dn_s[rs, :].astype(F32)).astype(BF16)
-            d_s[rs, :] = (dmid_s[rs, :].astype(F32) + dh.astype(F32)).astype(BF16)
-            if i % 4 == 3 and i // 4 < 3:
-                wg_qkv(i // 4)
-        hook(4)
+            r = rms_scale(xf)
+            dh = norm_back(xf, r, dn_s[rs, :].astype(F32)).astype(BF16)
+            x_s[l, rs, :] = (xf * r).astype(BF16)
+            d_s[rs, :] = (dmid_s[l, rs, :].astype(F32) + dh.astype(F32)).astype(BF16)
 
     def bwd_body(i, carry):
-        bwd(n_layers - 1 - i, lambda n: None)
+        l = n_layers - 1 - i
+        gelu_phase(l, lambda n: None)
+        mid_phase(l)
+        attn_phase(l)
+        in_phase(l)
         return carry
 
     lax.fori_loop(0, n_layers - 1, bwd_body, 0)
@@ -397,28 +399,80 @@
         for j in range(5, 12):
             cs[j](k).wait_send()
 
-    def hook(n):
-        if n == 0:
-            loop(s0, 0, n_dn)
-        elif n == 1:
-            loop(s1, 0, n_dn)
-        elif n == 2:
-            loop(s0, n_dn, k_o + 1)
-        elif n == 3:
-            loop(s1, n_dn, k_o + 1)
-        elif n == 4:
-            loop(s0, k_q, n_chunk)
-
-    bwd(0, hook)
+    first = n_layers - 1
+
+    def put(l, k, sl, val):
+        if l == first:
+            acc[(k, *sl)] = val
+        else:
+            acc[(k, *sl)] += val
+
+    def wg_up(l, m):
+        for n0, nn in fb:
+            res = mmg(m, z_s[l, :, n0:n0 + nn], TN)
+            for t in range(0, nn, 128):
+                r = n0 + t
+                put(l, n_dn + r // dm, (slice(None), slice(r % dm, r % dm + 128)), res[:, t:t + 128])
+
+    def wg_o(l):
+        put(l, k_o, (slice(None), slice(None)), mmg(mix_s[l], dmid_s[l], TN))
+
+    def wg_qkv(l):
+        for i in range(3):
+            put(l, k_q + i, (slice(None), slice(None)), mmg(qkv_s[l, :, i * dm:(i + 1) * dm], x_s[l], TN))
+
+    def after(i):
+        done = min((i + 1) * BLOCK // dm, n_dn)
+        prev = i * BLOCK // dm
+        for k in range(prev, done):
+            s0(k)
+        if i >= 1:
+            for k in range((i - 1) * BLOCK // dm, prev):
+                s1(k)
+
+    for r_0, rn in rows:
+        rs = slice(r_0, r_0 + rn)
+        hf = h_s[0, rs, :].astype(F32)
+        u_s[rs, :] = (hf * rms_scale(hf)).astype(BF16)
+    gelu_phase(0, after)
+    order = list(range(first, -1, -1))
+    for i, l in enumerate(order):
+        wg_up(l, h_s[l] if l else u_s[...])
+        if i == 0:
+            loop(s1, n_dn - 1, n_dn)
+        if i >= 3:
+            loop(s2, i - 3, i - 2)
+    loop(s0, n_dn, 2 * n_dn)
+    loop(s2, 3, n_dn)
+    mid_phase(0)
+    loop(s1, n_dn, 2 * n_dn)
+    attn_phase(0)
+    loop(g2, 0, n_dn)
+    in_phase(0)
     dx_ref[...] = d_s[...]
+    loop(s2, n_dn, 2 * n_dn)
+    for l in order:
+        wg_o(l)
+    loop(s0, k_o, k_o + 1)
+    loop(g1, 0, n_dn)
+    for i, l in enumerate(order):
+        wg_qkv(l)
+        if i == 1:
+            loop(s1, k_o, k_o + 1)
+        if i == 3:
+            loop(g2, n_dn, 2 * n_dn)
+    loop(s0, k_q, n_chunk)
     loop(s1, k_q, n_chunk)
-    loop(s2)
     loop(lambda k: cs[0](k).wait_send())
     pl.semaphore_signal(free_sem, inc=1, device_id=(cp,), device_id_type=MESH)
-    loop(g2)
-    loop(g1)
+    loop(g1, n_dn, 2 * n_dn)
+    loop(s2, 2 * n_dn, n_chunk)
     pl.semaphore_wait(free_sem, 1)
-    loop(g0)
+    loop(g0, 0, n_dn)
+    loop(g2, 2 * n_dn, n_chunk)
+    loop(g0, n_dn, 2 * n_dn)
+    loop(g1, 2 * n_dn, n_chunk)
+    loop(g0, 2 * n_dn, n_chunk)
     loop(finish)
 
 
@@ -472,11 +526,11 @@
                 pltpu.VMEM((n_layers, tok, ff), BF16),
                 pltpu.VMEM((tok, dm), BF16),
                 pltpu.VMEM((tok, ff), BF16),
-                pltpu.VMEM((tok, ff), BF16),
-                pltpu.VMEM((tok, dm), BF16),
-                pltpu.VMEM((tok, 3 * dm), BF16),
+                pltpu.VMEM((2, tok, BLOCK), BF16),
+                pltpu.VMEM((tok, dm), F32),
                 pltpu.VMEM((tok, dm), BF16),
                 pltpu.VMEM((tok, dm), BF16),
+                pltpu.VMEM((n_layers, tok, dm), BF16),
                 pltpu.VMEM((n_seq * n_pair, 2 * seq, seq), BF16),
                 pltpu.VMEM((n_chunk, dm // 2, dm), F32),
                 pltpu.VMEM((n_chunk, dm // 8, dm), F32),

time: 141 us -> 133 us (0.943)
  Pallas kernels: 140 us -> 132 us
    pallas_call x1, Pallas kernels: 137 us -> 129 us  [per_device(): pl.pallas_call(functools.partial(block_kernel, n_seq, seq, n_layers, n_he...]
where the time goes in v3:
time: 133 us
  Pallas kernels  132 us (99%)
    pallas_call x1, Pallas kernels, per_device(): pl.pallas_call(functools.partial(block_kernel, n_seq, seq, n_layers, n_he...  129 us
    pallas_call x1, Pallas kernels, per_device(): pl.pallas_call(store_kernel, out_shape=(sq, sq, sq, sq, jax.ShapeDtypeStr...  3.12 us

profile of v3, /device:TPU:0, one launch (start us, length us, event | category | flops | bytes accessed | tf_op | source)
XLA Modules:
  0.0 132.6 jit_solution(927888752998200860)
XLA Ops:
  0.6 128.6 %shard_map.144 = (f32[12,384,384]{2,1,0:T(8,128)S(1)}, bf16[512,384]{1,0:T(8,128)(2,1)S(1)}) custom-call(bf16[512,384]{1,0:T(8,128)(2,1)} %bitcast.23, bf16[512,384]{1,0:T(8,128)(2,1)} %bitcast.24, bf16[6,384]{1,0:T(8,128)(2,1)} %emb_ref.1, bf16[384,384]{1,0:T(8,128)(2,1)} %bitcast.25, bf16[384,384]{1,0:T(8,128)(2,1)} %bitcast.26, ...), custom_call_target="tpu_custom_call" | custom-call | tf_op jit(solution)/shard_map/pallas_call | solution.py:506
  129.3 3.1 %shard_map.145 = (f32[384,384]{1,0:T(8,128)}, f32[384,384]{1,0:T(8,128)}, f32[384,384]{1,0:T(8,128)}, f32[384,384]{1,0:T(8,128)}, f32[384,1536]{1,0:T(8,128)}, /...) custom-call(f32[12,384,384]{2,1,0:T(8,128)S(1)} %get-tuple-element.16.acc, bf16[512,384]{1,0:T(8,128)(2,1)S(1)} %get-tuple-element.17.dx_ref), custom_call_target="tpu_custom_call" | custom-call | tf_op jit(solution)/shard_map/pallas_call | solution.py:550

commit v4 on v3

--- a/solution.py
+++ b/solution.py
@@ -42,12 +42,23 @@
     return dy * r - xf * (r * r * r * inner)
 
 
+def merge(*streams):
+    plan = []
+    for si, (start, steps) in enumerate(streams):
+        at = start
+        for cost, fn in steps:
+            plan.append((at, si, fn))
+            at += cost
+    for _, _, fn in sorted(plan, key=lambda e: e[:2]):
+        fn()
+
+
 def block_kernel(n_seq, seq, n_layers, n_heads,
                  x_hbm, g_hbm, emb_ref, wq_hbm, wk_hbm, wv_hbm, wo_hbm, wup_hbm, wdn_hbm,
                  acc, dx_ref,
                  wqkv_s, wqkvt_s, wo_s, wot_s, wup_s, wupt_s, wdn_s, wdnt_s, emb_s,
                  x_s, qkv_s, p_s, mix_s, h_s, z_s,
-                 u_s, g_s, da_s, yp_s, dn_s, d_s, dmid_s, st_s,
+                 u_s, g_s, da_s, dn_s, d_s, dmid_s, st_s,
                  r0, ra, rb, ra2, rb2, in_sem, ssem, rsem, free_sem):
     tok, dm = d_s.shape
     ff = wup_s.shape[1]
@@ -105,89 +116,109 @@
     def seq_rows(s):
         return slice(s * seq, (s + 1) * seq)
 
-    def fwd(l, carry):
+    hrows = tok // 2
+    hseq = n_seq // 2
+
+    def sub_rows(h, rb):
+        return [slice(h * hrows + r_0, h * hrows + r_0 + rn) for r_0, rn in blocks(hrows, rb)]
+
+    def col_blocks(n):
+        return [slice(n0, n0 + nn) for n0, nn in blocks(n, NB)]
+
+    def fwd_half(l, h):
+        hr = slice(h * hrows, (h + 1) * hrows)
         emb_l = emb_s[l]
-        tl = ff // n_layers
-        ts = pl.ds(pl.multiple_of(l * tl, tl), tl)
-        wupt_s[ts, :] = wup_s[:, ts].T
-        wdnt_s[:, ts] = wdn_s[ts, :].T
-        for r_0, rn in rows:
-            rs = slice(r_0, r_0 + rn)
+        steps = []
+
+        def start(rs):
             xb = (d_s[rs, :].astype(F32) + emb_l).astype(BF16)
             x_s[l, rs, :] = xb
             xf = xb.astype(F32)
             u_s[rs, :] = (xf * rms_scale(xf)).astype(BF16)
-        for n0, nn in blocks(3 * dm, NB):
-            ns = slice(n0, n0 + nn)
-            qkv_s[l, :, ns] = mm(u_s[...], wqkv_s[:, ns]).astype(BF16)
-
-        def scores(s):
+
+        def qkv(ns):
+            qkv_s[l, hr, ns] = mm(u_s[hr, :], wqkv_s[:, ns]).astype(BF16)
+
+        def scores(s, j):
             rs = seq_rows(s)
-            for j in range(n_pair):
-                cc = j * pw
-                k = stack(qkv_s[l, rs, dm + cc:dm + cc + pw])
-                st_s[s * n_pair + j] = mmg(k, qkv_s[l, rs, cc:cc + pw], NT).astype(BF16)
-
-        def soft(s):
-            for j in range(n_pair):
-                for i, half in enumerate(halves(st_s[s * n_pair + j])):
-                    sf = half.astype(F32)
-                    top = jnp.max(sf, axis=0, keepdims=True)
-                    e = jnp.exp2((sf - top) * (scale * LOG2E))
-                    pr = e * (1.0 / jnp.sum(e, axis=0, keepdims=True))
-                    p_s[l, s * n_pair + j, i * seq:(i + 1) * seq, :] = pr
-
-        def mix(s):
+            cc = j * pw
+            k = stack(qkv_s[l, rs, dm + cc:dm + cc + pw])
+            st_s[s * n_pair + j] = mmg(k, qkv_s[l, rs, cc:cc + pw], NT).astype(BF16)
+
+        def soft(s, j):
+            for i, half in enumerate(halves(st_s[s * n_pair + j])):
+                sf = half.astype(F32)
+                top = jnp.max(sf, axis=0, keepdims=True)
+                e = jnp.exp2((sf - top) * (scale * LOG2E))
+                pr = e * (1.0 / jnp.sum(e, axis=0, keepdims=True))
+                p_s[l, s * n_pair + j, i * seq:(i + 1) * seq, :] = pr
+
+        def mix(s, j):
             rs = seq_rows(s)
-            for j in range(n_pair):
-                cc = j * pw
-                v = stack(qkv_s[l, rs, 2 * dm + cc:2 * dm + cc + pw])
-                pb = p_s[l, s * n_pair + j].astype(BF16)
-                mix_s[l, rs, cc:cc + pw] = mmg(pb, v, TN).astype(BF16)
-
-        for s in range(n_seq + 2):
-            if s < n_seq:
-                scores(s)
-            if 1 <= s <= n_seq:
-                soft(s - 1)
-            if s >= 2:
-                mix(s - 2)
-        for n0, nn in blocks(dm, NB):
-            ns = slice(n0, n0 + nn)
-            o = mm(mix_s[l], wo_s[:, ns]).astype(BF16)
-            h_s[l, :, ns] = (x_s[l, :, ns].astype(F32) + o.astype(F32)).astype(BF16)
-        for r_0, rn in rows:
-            rs = slice(r_0, r_0 + rn)
+            cc = j * pw
+            v = stack(qkv_s[l, rs, 2 * dm + cc:2 * dm + cc + pw])
+            pb = p_s[l, s * n_pair + j].astype(BF16)
+            mix_s[l, rs, cc:cc + pw] = mmg(pb, v, TN).astype(BF16)
+
+        def out(ns):
+            o = mm(mix_s[l, hr, :], wo_s[:, ns]).astype(BF16)
+            h_s[l, hr, ns] = (x_s[l, hr, ns].astype(F32) + o.astype(F32)).astype(BF16)
+
+        def norm2(rs):
             hf = h_s[l, rs, :].astype(F32)
             u_s[rs, :] = (hf * rms_scale(hf)).astype(BF16)
-        def up(i):
-            n0, nn = fb[i]
-            ns = slice(n0, n0 + nn)
-            z_s[l, :, ns] = mm(u_s[...], wup_s[:, ns]).astype(BF16)
-
-        def gelu(i):
-            n0, nn = fb[i]
-            ns = slice(n0, n0 + nn)
-            for r_0, rn in rows:
-                rs = slice(r_0, r_0 + rn)
-                z = z_s[l, rs, ns].astype(F32)
-                cdf = 0.5 + 0.5 * jnp.tanh(z * (GC0 + GC1 * (z * z)))
-                g_s[rs, ns] = (z * cdf).astype(BF16)
-
-        half = len(fb) // 2 * BLOCK
-        up(0)
-        for i in range(len(fb)):
-            if i + 1 < len(fb):
-                up(i + 1)
-            gelu(i)
-            if i + 1 == len(fb) - 1:
-                for n0, nn in blocks(dm, NB):
-                    ns = slice(n0, n0 + nn)
-                    yp_s[:, ns] = mm(g_s[:, :half], wdn_s[:half, ns])
-        for n0, nn in blocks(dm, NB):
-            ns = slice(n0, n0 + nn)
-            yd = (yp_s[:, ns] + mm(g_s[:, half:], wdn_s[half:, ns])).astype(BF16)
-            d_s[:, ns] = (h_s[l, :, ns].astype(F32) + yd.astype(F32)).astype(BF16)
+
+        def up(ns):
+            z_s[l, hr, ns] = mm(u_s[hr, :], wup_s[:, ns]).astype(BF16)
+
+        def gelu(rs, ns):
+            z = z_s[l, rs, ns].astype(F32)
+            cdf = 0.5 + 0.5 * jnp.tanh(z * (GC0 + GC1 * (z * z)))
+            g_s[rs, ns] = (z * cdf).astype(BF16)
+
+        def down(ns):
+            yd = mm(g_s[hr, :], wdn_s[:, ns]).astype(BF16)
+            d_s[hr, ns] = (h_s[l, hr, ns].astype(F32) + yd.astype(F32)).astype(BF16)
+
+        def step(cost, fn, *args):
+            steps.append((cost, functools.partial(fn, *args)))
+
+        for rs in sub_rows(h, 64):
+            step(60, start, rs)
+        for ns in col_blocks(3 * dm):
+            step(120, qkv, ns)
+        pairs = [(h * hseq + s, j) for s in range(hseq) for j in range(n_pair)]
+        for t in range(len(pairs) + 3):
+            if t < len(pairs):
+                step(40, scores, *pairs[t])
+            if 1 <= t <= len(pairs):
+                step(70, soft, *pairs[t - 1])
+            if t >= 3:
+                step(50, mix, *pairs[t - 3])
+        for ns in col_blocks(dm):
+            step(100, out, ns)
+        for rs in sub_rows(h, 64):
+            step(70, norm2, rs)
+        cols = col_blocks(ff)
+        step(100, up, cols[0])
+        for i, ns in enumerate(cols):
+            if i + 1 < len(cols):
+                step(20, up, cols[i + 1])
+            for rs in sub_rows(h, 64):
+                step(38, gelu, rs, ns)
+        for ns in col_blocks(dm):
+            step(380, down, ns)
+        return steps
+
+    def fwd(l, carry):
+        tl = ff // n_layers
+        ts = pl.ds(pl.multiple_of(l * tl, tl), tl)
+
+        def wt():
+            wupt_s[ts, :] = wup_s[:, ts].T
+            wdnt_s[:, ts] = wdn_s[ts, :].T
+
+        merge((0, fwd_half(l, 0)), (400, fwd_half(l, 1)), (2500, [(1, wt)]))
         return carry
 
     lax.fori_loop(0, n_layers, fwd, 0)
@@ -371,13 +402,17 @@
         cs[3](k).start()
         cs[4](k).start()
 
-    def g2(k):
+    def g2(k, both=True):
         cs[3](k).wait_recv()
         add(k, a1, h3, ra2)
         cs[4](k).wait_recv()
         add(k, b1, h3, rb2)
-        for j in (5, 6, 7, 8):
+        for j in (5, 6, 7, 8) if both else (5, 6):
             cs[j](k).start()
+
+    def g2_own(k):
+        cs[7](k).start()
+        cs[8](k).start()
 
     def g1(k):
         cs[5](k).wait_recv()
@@ -469,7 +504,8 @@
     loop(s2, 2 * n_dn, n_chunk)
     pl.semaphore_wait(free_sem, 1)
     loop(g0, 0, n_dn)
-    loop(g2, 2 * n_dn, n_chunk)
+    loop(lambda k: g2(k, False), 2 * n_dn, n_chunk)
+    loop(g2_own, 2 * n_dn, n_chunk)
     loop(g0, n_dn, 2 * n_dn)
     loop(g1, 2 * n_dn, n_chunk)
     loop(g0, 2 * n_dn, n_chunk)
@@ -527,7 +563,6 @@
                 pltpu.VMEM((tok, dm), BF16),
                 pltpu.VMEM((tok, ff), BF16),
                 pltpu.VMEM((2, tok, BLOCK), BF16),
-                pltpu.VMEM((tok, dm), F32),
                 pltpu.VMEM((tok, dm), BF16),
                 pltpu.VMEM((tok, dm), BF16),
                 pltpu.VMEM((n_layers, tok, dm), BF16),

time: 133 us -> 131 us (0.985)
  Pallas kernels: 132 us -> 130 us
    pallas_call x1, Pallas kernels: 129 us -> 127 us  [per_device(): pl.pallas_call(functools.partial(block_kernel, n_seq, seq, n_layers, n_he...]
where the time goes in v4:
time: 131 us
  Pallas kernels  130 us (99%)
    pallas_call x1, Pallas kernels, per_device(): pl.pallas_call(functools.partial(block_kernel, n_seq, seq, n_layers, n_he...  127 us
    pallas_call x1, Pallas kernels, per_device(): pl.pallas_call(store_kernel, out_shape=(sq, sq, sq, sq, jax.ShapeDtypeStr...  3.12 us

profile of v4, /device:TPU:0, one launch (start us, length us, event | category | flops | bytes accessed | tf_op | source)
XLA Modules:
  0.0 130.8 jit_solution(12377267462708143374)
XLA Ops:
  0.6 126.8 %shard_map.144 = (f32[12,384,384]{2,1,0:T(8,128)S(1)}, bf16[512,384]{1,0:T(8,128)(2,1)S(1)}) custom-call(bf16[512,384]{1,0:T(8,128)(2,1)} %bitcast.23, bf16[512,384]{1,0:T(8,128)(2,1)} %bitcast.24, bf16[6,384]{1,0:T(8,128)(2,1)} %emb_ref.1, bf16[384,384]{1,0:T(8,128)(2,1)} %bitcast.25, bf16[384,384]{1,0:T(8,128)(2,1)} %bitcast.26, ...), custom_call_target="tpu_custom_call" | custom-call | tf_op jit(solution)/shard_map/pallas_call | solution.py:542
  127.5 3.1 %shard_map.145 = (f32[384,384]{1,0:T(8,128)}, f32[384,384]{1,0:T(8,128)}, f32[384,384]{1,0:T(8,128)}, f32[384,384]{1,0:T(8,128)}, f32[384,1536]{1,0:T(8,128)}, /...) custom-call(f32[12,384,384]{2,1,0:T(8,128)S(1)} %get-tuple-element.16.acc, bf16[512,384]{1,0:T(8,128)(2,1)S(1)} %get-tuple-element.17.dx_ref), custom_call_target="tpu_custom_call" | custom-call | tf_op jit(solution)/shard_map/pallas_call | solution.py:585

commit v5 on v4

--- a/solution.py
+++ b/solution.py
@@ -54,9 +54,9 @@
 
 
 def block_kernel(n_seq, seq, n_layers, n_heads,
-                 x_hbm, g_hbm, emb_ref, wq_hbm, wk_hbm, wv_hbm, wo_hbm, wup_hbm, wdn_hbm,
+                 x_hbm, g_hbm, emb_hbm, wq_hbm, wk_hbm, wv_hbm, wo_hbm, wup_hbm, wdn_hbm,
                  acc, dx_ref,
-                 wqkv_s, wqkvt_s, wo_s, wot_s, wup_s, wupt_s, wdn_s, wdnt_s, emb_s,
+                 wqkv_s, wqkvt_s, wo_s, wot_s, wup_s, wupt_s, wdn_s, wdnt_s, emb_s, embb_s,
                  x_s, qkv_s, p_s, mix_s, h_s, z_s,
                  u_s, g_s, da_s, dn_s, d_s, dmid_s, st_s,
                  r0, ra, rb, ra2, rb2, in_sem, ssem, rsem, free_sem):
@@ -87,18 +87,18 @@
 
     loads = [pltpu.make_async_copy(src, dst, in_sem.at[i]) for i, (src, dst) in enumerate((
         (wq_hbm, wqkvt_s.at[0:dm, :]), (wk_hbm, wqkvt_s.at[dm:2 * dm, :]), (wv_hbm, wqkvt_s.at[2 * dm:3 * dm, :]),
-        (x_hbm, d_s), (wo_hbm, wo_s), (wup_hbm, wup_s), (wdn_hbm, wdn_s), (g_hbm, dmid_s.at[0])))]
+        (x_hbm, d_s), (wo_hbm, wo_s), (wup_hbm, wup_s), (wdn_hbm, wdn_s), (g_hbm, dmid_s.at[0]), (emb_hbm, embb_s)))]
     for ld in loads:
         ld.start()
-    emb = emb_ref[...].astype(F32)
-    for l in range(n_layers):
-        emb_s[l] = emb[l:l + 1]
     acc[0:n_dn] = jnp.zeros((n_dn, dm, dm), F32)
     for i in range(3):
         loads[i].wait()
         wqkv_s[:, i * dm:(i + 1) * dm] = wqkvt_s[i * dm:(i + 1) * dm, :].T
     for ld in loads[3:]:
         ld.wait()
+    emb = embb_s[...].astype(F32)
+    for l in range(n_layers):
+        emb_s[l] = emb[l:l + 1]
     wot_s[...] = wo_s[...].T
 
     low = lax.broadcasted_iota(jnp.int32, (seq, pw), 1) < hd
@@ -218,7 +218,7 @@
             wupt_s[ts, :] = wup_s[:, ts].T
             wdnt_s[:, ts] = wdn_s[ts, :].T
 
-        merge((0, fwd_half(l, 0)), (400, fwd_half(l, 1)), (2500, [(1, wt)]))
+        merge((0, fwd_half(l, 0)), (700, fwd_half(l, 1)), (2500, [(1, wt)]))
         return carry
 
     lax.fori_loop(0, n_layers, fwd, 0)
@@ -232,7 +232,7 @@
         def gelu_back(i):
             n0, nn = fb[i]
             ns = slice(n0, n0 + nn)
-            for r_0, rn in rows_b:
+            for r_0, rn in blocks(tok, 32):
                 rs = slice(r_0, r_0 + rn)
                 z = z_s[l, rs, ns].astype(F32)
                 z2 = z * z
@@ -264,7 +264,7 @@
         for n0, nn in blocks(dm, NB):
             ns = slice(n0, n0 + nn)
             dn_s[:, ns] = mm(z_s[l], wupt_s[:, ns]).astype(BF16)
-        for r_0, rn in rows_b:
+        for r_0, rn in blocks(tok, 32):
             rs = slice(r_0, r_0 + rn)
             hf = h_s[l, rs, :].astype(F32)
             r = rms_scale(hf)
@@ -275,52 +275,56 @@
     def attn_phase(l):
         for n0, nn in blocks(dm, NB):
             ns = slice(n0, n0 + nn)
-            dn_s[:, ns] = mm(dmid_s[l], wot_s[:, ns]).astype(BF16)
-
-        def dprob(s):
+            dn_s[:tok // 2, ns] = mm(dmid_s[l, :tok // 2], wot_s[:, ns]).astype(BF16)
+        for n0, nn in blocks(dm, NB):
+            ns = slice(n0, n0 + nn)
+            dn_s[tok // 2:, ns] = mm(dmid_s[l, tok // 2:], wot_s[:, ns]).astype(BF16)
+
+        def dprob(s, j):
             rs = seq_rows(s)
-            for j in range(n_pair):
-                cc = j * pw
-                v = stack(qkv_s[l, rs, 2 * dm + cc:2 * dm + cc + pw])
-                st_s[s * n_pair + j] = mmg(v, dn_s[rs, cc:cc + pw], NT).astype(BF16)
-
-        def dscore(s):
-            for j in range(n_pair):
-                i = s * n_pair + j
-                for hh in range(2):
-                    hs = slice(hh * seq, (hh + 1) * seq)
-                    pf = p_s[l, i, hs, :]
-                    dp = st_s[i, hs, :].astype(F32)
-                    inner = jnp.sum(pf * dp, axis=0, keepdims=True)
-                    st_s[i, hs, :] = (pf * (dp - inner) * scale).astype(BF16)
-
-        def dqkv(s):
+            cc = j * pw
+            v = stack(qkv_s[l, rs, 2 * dm + cc:2 * dm + cc + pw])
+            st_s[s * n_pair + j] = mmg(v, dn_s[rs, cc:cc + pw], NT).astype(BF16)
+
+        def dscore(s, j):
+            i = s * n_pair + j
+            for hh in range(2):
+                hs = slice(hh * seq, (hh + 1) * seq)
+                pf = p_s[l, i, hs, :]
+                dp = st_s[i, hs, :].astype(F32)
+                inner = jnp.sum(pf * dp, axis=0, keepdims=True)
+                st_s[i, hs, :] = (pf * (dp - inner) * scale).astype(BF16)
+
+        def dqkv(s, j):
             rs = seq_rows(s)
-            for j in range(n_pair):
-                i = s * n_pair + j
-                cc = j * pw
-                dst = st_s[i]
-                q = stack(qkv_s[l, rs, cc:cc + pw])
-                k = stack(qkv_s[l, rs, dm + cc:dm + cc + pw])
-                dmx = stack(dn_s[rs, cc:cc + pw])
-                qkv_s[l, rs, cc:cc + pw] = mmg(dst, k, TN).astype(BF16)
-                qkv_s[l, rs, dm + cc:dm + cc + pw] = mm(beside(dst), q).astype(BF16)
-                pb = p_s[l, i].astype(BF16)
-                qkv_s[l, rs, 2 * dm + cc:2 * dm + cc + pw] = mm(beside(pb), dmx).astype(BF16)
-
-        for s in range(n_seq + 2):
-            if s < n_seq:
-                dprob(s)
-            if 1 <= s <= n_seq:
-                dscore(s - 1)
-            if s >= 2:
-                dqkv(s - 2)
+            i = s * n_pair + j
+            cc = j * pw
+            dst = st_s[i]
+            q = stack(qkv_s[l, rs, cc:cc + pw])
+            k = stack(qkv_s[l, rs, dm + cc:dm + cc + pw])
+            dmx = stack(dn_s[rs, cc:cc + pw])
+            qkv_s[l, rs, cc:cc + pw] = mmg(dst, k, TN).astype(BF16)
+            qkv_s[l, rs, dm + cc:dm + cc + pw] = mm(beside(dst), q).astype(BF16)
+            pb = p_s[l, i].astype(BF16)
+            qkv_s[l, rs, 2 * dm + cc:2 * dm + cc + pw] = mm(beside(pb), dmx).astype(BF16)
+
+        pairs = [(s, j) for s in range(n_seq) for j in range(n_pair)]
+        for t in range(len(pairs) + 3):
+            if t < len(pairs):
+                dprob(*pairs[t])
+            if 1 <= t < len(pairs) + 1:
+                dscore(*pairs[t - 1])
+            if t >= 3:
+                dqkv(*pairs[t - 3])
 
     def in_phase(l):
         for n0, nn in blocks(dm, NB):
             ns = slice(n0, n0 + nn)
-            dn_s[:, ns] = mm(qkv_s[l], wqkvt_s[:, ns]).astype(BF16)
-        for r_0, rn in rows_b:
+            dn_s[:tok // 2, ns] = mm(qkv_s[l, :tok // 2], wqkvt_s[:, ns]).astype(BF16)
+        for n0, nn in blocks(dm, NB):
+            ns = slice(n0, n0 + nn)
+            dn_s[tok // 2:, ns] = mm(qkv_s[l, tok // 2:], wqkvt_s[:, ns]).astype(BF16)
+        for r_0, rn in blocks(tok, 32):
             rs = slice(r_0, r_0 + rn)
             xf = x_s[l, rs, :].astype(F32)
             r = rms_scale(xf)
@@ -542,7 +546,7 @@
         acc, dx = pl.pallas_call(
             functools.partial(block_kernel, n_seq, seq, n_layers, n_heads),
             out_shape=(pltpu.VMEM((n_chunk, dm, dm), F32), pltpu.VMEM((tok, dm), BF16)),
-            in_specs=[hb, hb, vm] + [hb] * 6,
+            in_specs=[hb] * 9,
             out_specs=[vm] * 2,
             scratch_shapes=[
                 pltpu.VMEM((dm, 3 * dm), BF16),
@@ -554,6 +558,7 @@
                 pltpu.VMEM((ff, dm), BF16),
                 pltpu.VMEM((dm, ff), BF16),
                 pltpu.VMEM((n_layers, 1, dm), F32),
+                pltpu.VMEM((n_layers, dm), BF16),
                 pltpu.VMEM((n_layers, tok, dm), BF16),
                 pltpu.VMEM((n_layers, tok, 3 * dm), BF16),
                 pltpu.VMEM((n_layers, n_seq * n_pair, 2 * seq, seq), F32),
@@ -572,7 +577,7 @@
                 pltpu.VMEM((n_chunk, dm // 8, dm), F32),
                 pltpu.VMEM((n_chunk, dm // 16, dm), F32),
                 pltpu.VMEM((n_chunk, dm // 16, dm), F32),
-                pltpu.SemaphoreType.DMA((8,)),
+                pltpu.SemaphoreType.DMA((9,)),
                 pltpu.SemaphoreType.DMA((12, n_chunk)),
                 pltpu.SemaphoreType.DMA((12, n_chunk)),
                 pltpu.SemaphoreType.REGULAR,

time: 131 us -> 128 us (0.977)
  Pallas kernels: 130 us -> 127 us
    pallas_call x1, Pallas kernels: 127 us -> 124 us  [per_device(): pl.pallas_call(functools.partial(block_kernel, n_seq, seq, n_layers, n_he...]
where the time goes in v5:
time: 128 us
  Pallas kernels  127 us (99%)
    pallas_call x1, Pallas kernels, per_device(): pl.pallas_call(functools.partial(block_kernel, n_seq, seq, n_layers, n_he...  124 us
    pallas_call x1, Pallas kernels, per_device(): pl.pallas_call(store_kernel, out_shape=(sq, sq, sq, sq, jax.ShapeDtypeStr...  3.12 us

profile of v5, /device:TPU:0, one launch (start us, length us, event | category | flops | bytes accessed | tf_op | source)
XLA Modules:
  0.0 128.2 jit_solution(13714642167786315205)
XLA Ops:
  0.6 124.2 %shard_map.144 = (f32[12,384,384]{2,1,0:T(8,128)S(1)}, bf16[512,384]{1,0:T(8,128)(2,1)S(1)}) custom-call(bf16[512,384]{1,0:T(8,128)(2,1)} %bitcast.23, bf16[512,384]{1,0:T(8,128)(2,1)} %bitcast.24, bf16[6,384]{1,0:T(8,128)(2,1)} %emb_hbm.1, bf16[384,384]{1,0:T(8,128)(2,1)} %bitcast.25, bf16[384,384]{1,0:T(8,128)(2,1)} %bitcast.26, ...), custom_call_target="tpu_custom_call" | custom-call | tf_op jit(solution)/shard_map/pallas_call | solution.py:546
  124.9 3.1 %shard_map.145 = (f32[384,384]{1,0:T(8,128)}, f32[384,384]{1,0:T(8,128)}, f32[384,384]{1,0:T(8,128)}, f32[384,384]{1,0:T(8,128)}, f32[384,1536]{1,0:T(8,128)}, /...) custom-call(f32[12,384,384]{2,1,0:T(8,128)S(1)} %get-tuple-element.16.acc, bf16[512,384]{1,0:T(8,128)(2,1)S(1)} %get-tuple-element.17.dx_ref), custom_call_target="tpu_custom_call" | custom-call | tf_op jit(solution)/shard_map/pallas_call | solution.py:590

commit v6 on v5

--- a/solution.py
+++ b/solution.py
@@ -195,7 +195,7 @@
                 step(70, soft, *pairs[t - 1])
             if t >= 3:
                 step(50, mix, *pairs[t - 3])
-        for ns in col_blocks(dm):
+        for ns in [slice(0, dm)]:
             step(100, out, ns)
         for rs in sub_rows(h, 64):
             step(70, norm2, rs)
@@ -203,10 +203,10 @@
         step(100, up, cols[0])
         for i, ns in enumerate(cols):
             if i + 1 < len(cols):
-                step(20, up, cols[i + 1])
+                step(120, up, cols[i + 1])
             for rs in sub_rows(h, 64):
                 step(38, gelu, rs, ns)
-        for ns in col_blocks(dm):
+        for ns in [slice(0, dm)]:
             step(380, down, ns)
         return steps
 
@@ -224,7 +224,7 @@
     lax.fori_loop(0, n_layers, fwd, 0)
     d_s[...] = dmid_s[0]
 
-    def gelu_phase(l, after):
+    def gelu_phase(l, after, lag=1):
         def dact(i):
             n0, nn = fb[i]
             da_s[i % 2] = mm(d_s[...], wdnt_s[:, n0:n0 + nn]).astype(BF16)
@@ -254,14 +254,15 @@
             if i + 1 < len(fb):
                 dact(i + 1)
             gelu_back(i)
-            if i >= 1:
-                wg_down(i - 1)
-                after(i - 1)
-        wg_down(len(fb) - 1)
-        after(len(fb) - 1)
+            if i >= lag:
+                wg_down(i - lag)
+                after(i - lag)
+        for i in range(len(fb) - lag, len(fb)):
+            wg_down(i)
+            after(i)
 
     def mid_phase(l):
-        for n0, nn in blocks(dm, NB):
+        for n0, nn in blocks(dm, dm):
             ns = slice(n0, n0 + nn)
             dn_s[:, ns] = mm(z_s[l], wupt_s[:, ns]).astype(BF16)
         for r_0, rn in blocks(tok, 32):
@@ -273,10 +274,10 @@
             dmid_s[l, rs, :] = (d_s[rs, :].astype(F32) + dh.astype(F32)).astype(BF16)
 
     def attn_phase(l):
-        for n0, nn in blocks(dm, NB):
+        for n0, nn in blocks(dm, dm):
             ns = slice(n0, n0 + nn)
             dn_s[:tok // 2, ns] = mm(dmid_s[l, :tok // 2], wot_s[:, ns]).astype(BF16)
-        for n0, nn in blocks(dm, NB):
+        for n0, nn in blocks(dm, dm):
             ns = slice(n0, n0 + nn)
             dn_s[tok // 2:, ns] = mm(dmid_s[l, tok // 2:], wot_s[:, ns]).astype(BF16)
 
@@ -309,19 +310,19 @@
             qkv_s[l, rs, 2 * dm + cc:2 * dm + cc + pw] = mm(beside(pb), dmx).astype(BF16)
 
         pairs = [(s, j) for s in range(n_seq) for j in range(n_pair)]
-        for t in range(len(pairs) + 3):
+        for t in range(len(pairs) + 4):
             if t < len(pairs):
                 dprob(*pairs[t])
             if 1 <= t < len(pairs) + 1:
                 dscore(*pairs[t - 1])
-            if t >= 3:
-                dqkv(*pairs[t - 3])
+            if t >= 4:
+                dqkv(*pairs[t - 4])
 
     def in_phase(l):
-        for n0, nn in blocks(dm, NB):
+        for n0, nn in blocks(dm, dm):
             ns = slice(n0, n0 + nn)
             dn_s[:tok // 2, ns] = mm(qkv_s[l, :tok // 2], wqkvt_s[:, ns]).astype(BF16)
-        for n0, nn in blocks(dm, NB):
+        for n0, nn in blocks(dm, dm):
             ns = slice(n0, n0 + nn)
             dn_s[tok // 2:, ns] = mm(qkv_s[l, tok // 2:], wqkvt_s[:, ns]).astype(BF16)
         for r_0, rn in blocks(tok, 32):
@@ -465,20 +466,20 @@
         prev = i * BLOCK // dm
         for k in range(prev, done):
             s0(k)
-        if i >= 1:
-            for k in range((i - 1) * BLOCK // dm, prev):
-                s1(k)
-
+        if i == len(fb) - 1:
+            s1(0)
+
+    gelu_phase(0, after, 0)
     for r_0, rn in rows:
         rs = slice(r_0, r_0 + rn)
         hf = h_s[0, rs, :].astype(F32)
         u_s[rs, :] = (hf * rms_scale(hf)).astype(BF16)
-    gelu_phase(0, after)
+    s1(1)
     order = list(range(first, -1, -1))
     for i, l in enumerate(order):
         wg_up(l, h_s[l] if l else u_s[...])
         if i == 0:
-            loop(s1, n_dn - 1, n_dn)
+            loop(s1, 2, n_dn)
         if i >= 3:
             loop(s2, i - 3, i - 2)
     loop(s0, n_dn, 2 * n_dn)

time: 128 us -> 128 us (level)
  no operation moved by 1% of the time
where the time goes in v6:
time: 128 us
  Pallas kernels  127 us (99%)
    pallas_call x1, Pallas kernels, per_device(): pl.pallas_call(functools.partial(block_kernel, n_seq, seq, n_layers, n_he...  124 us
    pallas_call x1, Pallas kernels, per_device(): pl.pallas_call(store_kernel, out_shape=(sq, sq, sq, sq, jax.ShapeDtypeStr...  3.12 us

profile of v6, /device:TPU:0, one launch (start us, length us, event | category | flops | bytes accessed | tf_op | source)
XLA Modules:
  0.0 127.9 jit_solution(10618336152266202759)
XLA Ops:
  0.6 123.9 %shard_map.144 = (f32[12,384,384]{2,1,0:T(8,128)S(1)}, bf16[512,384]{1,0:T(8,128)(2,1)S(1)}) custom-call(bf16[512,384]{1,0:T(8,128)(2,1)} %bitcast.23, bf16[512,384]{1,0:T(8,128)(2,1)} %bitcast.24, bf16[6,384]{1,0:T(8,128)(2,1)} %emb_hbm.1, bf16[384,384]{1,0:T(8,128)(2,1)} %bitcast.25, bf16[384,384]{1,0:T(8,128)(2,1)} %bitcast.26, ...), custom_call_target="tpu_custom_call" | custom-call | tf_op jit(solution)/shard_map/pallas_call | solution.py:547
  124.5 3.1 %shard_map.145 = (f32[384,384]{1,0:T(8,128)}, f32[384,384]{1,0:T(8,128)}, f32[384,384]{1,0:T(8,128)}, f32[384,384]{1,0:T(8,128)}, f32[384,1536]{1,0:T(8,128)}, /...) custom-call(f32[12,384,384]{2,1,0:T(8,128)S(1)} %get-tuple-element.16.acc, bf16[512,384]{1,0:T(8,128)(2,1)S(1)} %get-tuple-element.17.dx_ref), custom_call_target="tpu_custom_call" | custom-call | tf_op jit(solution)/shard_map/pallas_call | solution.py:591

commit v7 on v6

--- a/solution.py
+++ b/solution.py
@@ -18,7 +18,7 @@
 NT = (((1,), (1,)), ((), ()))
 TN = (((0,), (0,)), ((), ()))
 VMEM_LIMIT = 58851328
-BLOCK = 256
+BLOCK = 512
 
 
 def mm(a, b):
@@ -70,7 +70,7 @@
     n_chunk = 2 * n_dn + 4
     k_o, k_q = 2 * n_dn, 2 * n_dn + 1
     scale = hd ** -0.5
-    NB = BLOCK
+    NB = 256
     rows = blocks(tok, 64)
     rows_b = blocks(tok, 32)
 

time: 128 us -> 129 us (level)
  no operation moved by 1% of the time
where the time goes in v7:
time: 129 us
  Pallas kernels  128 us (99%)
    pallas_call x1, Pallas kernels, per_device(): pl.pallas_call(functools.partial(block_kernel, n_seq, seq, n_layers, n_he...  125 us
    pallas_call x1, Pallas kernels, per_device(): pl.pallas_call(store_kernel, out_shape=(sq, sq, sq, sq, jax.ShapeDtypeStr...  3.12 us

profile of v7, /device:TPU:0, one launch (start us, length us, event | category | flops | bytes accessed | tf_op | source)
XLA Modules:
  0.0 128.5 jit_solution(4029322640950257673)
XLA Ops:
  0.6 124.6 %shard_map.144 = (f32[12,384,384]{2,1,0:T(8,128)S(1)}, bf16[512,384]{1,0:T(8,128)(2,1)S(1)}) custom-call(bf16[512,384]{1,0:T(8,128)(2,1)} %bitcast.23, bf16[512,384]{1,0:T(8,128)(2,1)} %bitcast.24, bf16[6,384]{1,0:T(8,128)(2,1)} %emb_hbm.1, bf16[384,384]{1,0:T(8,128)(2,1)} %bitcast.25, bf16[384,384]{1,0:T(8,128)(2,1)} %bitcast.26, ...), custom_call_target="tpu_custom_call" | custom-call | tf_op jit(solution)/shard_map/pallas_call | solution.py:547
  125.2 3.1 %shard_map.145 = (f32[384,384]{1,0:T(8,128)}, f32[384,384]{1,0:T(8,128)}, f32[384,384]{1,0:T(8,128)}, f32[384,384]{1,0:T(8,128)}, f32[384,1536]{1,0:T(8,128)}, /...) custom-call(f32[12,384,384]{2,1,0:T(8,128)S(1)} %get-tuple-element.16.acc, bf16[512,384]{1,0:T(8,128)(2,1)S(1)} %get-tuple-element.17.dx_ref), custom_call_target="tpu_custom_call" | custom-call | tf_op jit(solution)/shard_map/pallas_call | solution.py:591

commit v8 on v6

--- a/solution.py
+++ b/solution.py
@@ -469,7 +469,7 @@
         if i == len(fb) - 1:
             s1(0)
 
-    gelu_phase(0, after, 0)
+    gelu_phase(0, after, 1)
     for r_0, rn in rows:
         rs = slice(r_0, r_0 + rn)
         hf = h_s[0, rs, :].astype(F32)

time: 128 us -> 128 us (level)
  no operation moved by 1% of the time
where the time goes in v8:
time: 128 us
  Pallas kernels  127 us (99%)
    pallas_call x1, Pallas kernels, per_device(): pl.pallas_call(functools.partial(block_kernel, n_seq, seq, n_layers, n_he...  124 us
    pallas_call x1, Pallas kernels, per_device(): pl.pallas_call(store_kernel, out_shape=(sq, sq, sq, sq, jax.ShapeDtypeStr...  3.12 us

profile of v8, /device:TPU:0, one launch (start us, length us, event | category | flops | bytes accessed | tf_op | source)
XLA Modules:
  0.0 127.9 jit_solution(6331454497274451888)
XLA Ops:
  0.6 124.0 %shard_map.144 = (f32[12,384,384]{2,1,0:T(8,128)S(1)}, bf16[512,384]{1,0:T(8,128)(2,1)S(1)}) custom-call(bf16[512,384]{1,0:T(8,128)(2,1)} %bitcast.23, bf16[512,384]{1,0:T(8,128)(2,1)} %bitcast.24, bf16[6,384]{1,0:T(8,128)(2,1)} %emb_hbm.1, bf16[384,384]{1,0:T(8,128)(2,1)} %bitcast.25, bf16[384,384]{1,0:T(8,128)(2,1)} %bitcast.26, ...), custom_call_target="tpu_custom_call" | custom-call | tf_op jit(solution)/shard_map/pallas_call | solution.py:547
  124.6 3.1 %shard_map.145 = (f32[384,384]{1,0:T(8,128)}, f32[384,384]{1,0:T(8,128)}, f32[384,384]{1,0:T(8,128)}, f32[384,384]{1,0:T(8,128)}, f32[384,1536]{1,0:T(8,128)}, /...) custom-call(f32[12,384,384]{2,1,0:T(8,128)S(1)} %get-tuple-element.16.acc, bf16[512,384]{1,0:T(8,128)(2,1)S(1)} %get-tuple-element.17.dx_ref), custom_call_target="tpu_custom_call" | custom-call | tf_op jit(solution)/shard_map/pallas_call | solution.py:591

commit v9 on v6

--- a/solution.py
+++ b/solution.py
@@ -87,14 +87,14 @@
 
     loads = [pltpu.make_async_copy(src, dst, in_sem.at[i]) for i, (src, dst) in enumerate((
         (wq_hbm, wqkvt_s.at[0:dm, :]), (wk_hbm, wqkvt_s.at[dm:2 * dm, :]), (wv_hbm, wqkvt_s.at[2 * dm:3 * dm, :]),
-        (x_hbm, d_s), (wo_hbm, wo_s), (wup_hbm, wup_s), (wdn_hbm, wdn_s), (g_hbm, dmid_s.at[0]), (emb_hbm, embb_s)))]
+        (x_hbm, d_s), (emb_hbm, embb_s), (wo_hbm, wo_s), (wup_hbm, wup_s), (wdn_hbm, wdn_s), (g_hbm, dmid_s.at[0])))]
     for ld in loads:
         ld.start()
     acc[0:n_dn] = jnp.zeros((n_dn, dm, dm), F32)
     for i in range(3):
         loads[i].wait()
         wqkv_s[:, i * dm:(i + 1) * dm] = wqkvt_s[i * dm:(i + 1) * dm, :].T
-    for ld in loads[3:]:
+    for ld in loads[3:-1]:
         ld.wait()
     emb = embb_s[...].astype(F32)
     for l in range(n_layers):
@@ -222,6 +222,7 @@
         return carry
 
     lax.fori_loop(0, n_layers, fwd, 0)
+    loads[-1].wait()
     d_s[...] = dmid_s[0]
 
     def gelu_phase(l, after, lag=1):

time: 128 us -> 128 us (level)
  no operation moved by 1% of the time
where the time goes in v9:
time: 128 us
  Pallas kernels  127 us (99%)
    pallas_call x1, Pallas kernels, per_device(): pl.pallas_call(functools.partial(block_kernel, n_seq, seq, n_layers, n_he...  124 us
    pallas_call x1, Pallas kernels, per_device(): pl.pallas_call(store_kernel, out_shape=(sq, sq, sq, sq, jax.ShapeDtypeStr...  3.12 us

profile of v9, /device:TPU:0, one launch (start us, length us, event | category | flops | bytes accessed | tf_op | source)
XLA Modules:
  0.0 127.8 jit_solution(18020178002158279360)
XLA Ops:
  0.6 123.9 %shard_map.144 = (f32[12,384,384]{2,1,0:T(8,128)S(1)}, bf16[512,384]{1,0:T(8,128)(2,1)S(1)}) custom-call(bf16[512,384]{1,0:T(8,128)(2,1)} %bitcast.23, bf16[512,384]{1,0:T(8,128)(2,1)} %bitcast.24, bf16[6,384]{1,0:T(8,128)(2,1)} %emb_hbm.1, bf16[384,384]{1,0:T(8,128)(2,1)} %bitcast.25, bf16[384,384]{1,0:T(8,128)(2,1)} %bitcast.26, ...), custom_call_target="tpu_custom_call" | custom-call | tf_op jit(solution)/shard_map/pallas_call | solution.py:548
  124.5 3.1 %shard_map.145 = (f32[384,384]{1,0:T(8,128)}, f32[384,384]{1,0:T(8,128)}, f32[384,384]{1,0:T(8,128)}, f32[384,384]{1,0:T(8,128)}, f32[384,1536]{1,0:T(8,128)}, /...) custom-call(f32[12,384,384]{2,1,0:T(8,128)S(1)} %get-tuple-element.16.acc, bf16[512,384]{1,0:T(8,128)(2,1)S(1)} %get-tuple-element.17.dx_ref), custom_call_target="tpu_custom_call" | custom-call | tf_op jit(solution)/shard_map/pallas_call | solution.py:592
